TPU v7x, 256 devices: a whole 4x4x8 slice. The times are simulated.
256 devices in a mesh: rep: 32 (over x_hi, z, core), tp: 8 (over x_lo, y).
Axes of the slice: x: 4 (x_hi: 2, x_lo: 2; x = x_hi * 2 + x_lo), y: 4, z: 8, core: 2. Of those that a mesh axis runs over, the one named last changes fastest.
Arguments:
- tokens: bfloat16 [32, 1024, 3072], P('rep', 'tp'), may hold values from -100 to 100
- norm_gain: float32 [32, 3072], P('rep'), may hold values from 0.5 to 1.5
- w_query: bfloat16 [32, 3072, 2048], P('rep', None, 'tp'), may hold values from -1 to 1
- key_weight: bfloat16 [32, 3072, 1024], P('rep', None, 'tp'), may hold values from -1 to 1
- value_weight: bfloat16 [32, 3072, 1024], P('rep', None, 'tp'), may hold values from -0.109375 to 0.109375
- attention_gradient: bfloat16 [32, 1024, 2048], P('rep', None, 'tp'), may hold values from -6 to 6
- global_fragment: float32 [512, 3072], P('tp'), may hold values from -6 to 6
- momentum: float32 [512, 3072], P('tp'), may hold values from -3 to 3
- local_fragment: bfloat16 [32, 512, 3072], P('rep', 'tp'), may hold values from -6 to 6
Outputs:
- grad_query_w: bfloat16 [32, 3072, 2048], P('rep', None, 'tp')
- grad_key_w: bfloat16 [32, 3072, 1024], P('rep', None, 'tp')
- grad_value_w: bfloat16 [32, 3072, 1024], P('rep', None, 'tp')
- grad_gain: float32 [32, 3072], P('rep')
- grad_tokens: bfloat16 [32, 1024, 3072], P('rep', 'tp')
- new_global: float32 [512, 3072], P('tp')
- new_momentum: float32 [512, 3072], P('tp')
All inputs are finite; a program needn't handle non-finite values.
Results may differ from a plain program's by a relative error of at most 0.019.
The roundings to bfloat16 on the way count: a program that leaves them out, or rounds other values in their place, can miss the bound.
Values may be sent and summed in bfloat16 or wider, within the bound.
A program may use at most 128 MiB of HBM per device.

v0:
```python
import jax
import jax.numpy as jnp
from jax import lax
from jax.sharding import PartitionSpec as P

HEAD_SIZE = 128


epsilon = 1e-05
rope_base = 500000.0
outer_rate = 0.7
outer_momentum = 0.9


def sent_to_all(value, axis):
    copies = jnp.broadcast_to(value, (lax.axis_size(axis), *value.shape))
    return lax.all_to_all(copies, axis, split_axis=0, concat_axis=0, tiled=True)


def of_everyone(value, axis):
    everything = sent_to_all(value, axis)
    return jnp.sum(everything, axis=0)


def cut_along(value, dim, size):
    before, after = (value.shape[:dim], value.shape[dim + 1 :])
    return jnp.moveaxis(value.reshape(*before, size, -1, *after), dim, 0)


def sent_and_summed(value, axis, dim):
    parts = cut_along(value, dim, lax.axis_size(axis))
    arrived = lax.all_to_all(parts, axis, split_axis=0, concat_axis=0, tiled=True)
    return arrived.sum(axis=0)


def in_one_piece(arrays, axis, dim, along):
    both = jnp.concatenate(arrays, axis=along)
    whole, at, done = (lax.all_gather(both, axis, axis=dim, tiled=True), 0, [])
    for a in arrays:
        done.append(lax.slice_in_dim(whole, at, at + a.shape[along], axis=along))
        at += a.shape[along]
    return tuple(done)


def rope_tables(sequence_length, width):
    middle = width // 2
    frequency = rope_base ** (-2.0 * jnp.arange(middle, dtype=jnp.float32) / width)
    angles = jnp.arange(sequence_length, dtype=jnp.float32)[:, None] * frequency[None, :]
    angles = jnp.concatenate([angles, angles], axis=1)
    return (jnp.cos(angles)[:, None, :], jnp.sin(angles)[:, None, :])


def rotate(vectors, cosine_table, sine_table):
    middle = vectors.shape[-1] // 2
    turned = jnp.concatenate([-vectors[..., middle:], vectors[..., :middle]], axis=-1)
    return vectors * cosine_table + turned * sine_table


def reverse_rotation(gradient, cosine_table, sine_table):
    middle = gradient.shape[-1] // 2
    shifted = gradient * sine_table
    turned = jnp.concatenate([shifted[..., middle:], -shifted[..., :middle]], axis=-1)
    return gradient * cosine_table + turned


def attention_reverse(query_rows, rotated_keys, values_bfloat, grad_out, block_of_rows):
    sequence_length = query_rows.shape[0]
    score_scale = query_rows.shape[-1] ** (-0.5)

    def one_block(running, block_index):
        acc_key, acc_value = running
        offset = block_index * block_of_rows
        query_block = lax.dynamic_slice_in_dim(query_rows, offset, block_of_rows, 0)
        grad_block = lax.dynamic_slice_in_dim(grad_out, offset, block_of_rows, 0)
        scores = (
            jnp.einsum(
                "qgrd,kgd->grqk", query_block, rotated_keys, preferred_element_type=jnp.float32
            )
            * score_scale
        )
        row_pos = offset + jnp.arange(block_of_rows)
        col_pos = jnp.arange(sequence_length)
        allowed = col_pos[None, :] <= row_pos[:, None]
        scores = jnp.where(allowed, scores, -jnp.inf)
        highest = jnp.max(scores, axis=-1, keepdims=True)
        powers = jnp.exp(scores - highest)
        probability = powers / jnp.sum(powers, axis=-1, keepdims=True)
        prob_low = probability.astype(jnp.bfloat16)
        acc_value = acc_value + jnp.einsum(
            "grqk,qgrd->kgd", prob_low, grad_block, preferred_element_type=jnp.float32
        )
        grad_prob = jnp.einsum(
            "qgrd,kgd->grqk", grad_block, values_bfloat, preferred_element_type=jnp.float32
        )
        grad_score = (
            probability
            * (grad_prob - jnp.sum(grad_prob * probability, axis=-1, keepdims=True))
            * score_scale
        )
        score_low = grad_score.astype(jnp.bfloat16)
        grad_query = jnp.einsum(
            "grqk,kgd->qgrd", score_low, rotated_keys, preferred_element_type=jnp.float32
        )
        acc_key = acc_key + jnp.einsum(
            "grqk,qgrd->kgd", score_low, query_block, preferred_element_type=jnp.float32
        )
        return ((acc_key, acc_value), grad_query)

    initial = jnp.zeros(rotated_keys.shape, jnp.float32)
    (acc_key, acc_value), grad_blocks = lax.scan(
        one_block, (initial, initial), jnp.arange(sequence_length // block_of_rows)
    )
    return (grad_blocks.reshape(query_rows.shape), acc_key, acc_value)


def body(
    tokens,
    norm_gain,
    w_query,
    key_weight,
    value_weight,
    attention_gradient,
    global_fragment,
    momentum,
    local_fragment,
):
    local_rows = tokens[0]
    norm_gains = norm_gain[0]
    weight_q = w_query[0]
    weight_k = key_weight[0]
    weight_v = value_weight[0]
    widened_rows = local_rows.astype(jnp.float32)
    inverse_norm = lax.rsqrt(
        jnp.mean(widened_rows * widened_rows, axis=-1, keepdims=True) + epsilon
    )
    normalized_input = widened_rows * inverse_norm
    normalized_local = (normalized_input * norm_gains[None, :]).astype(jnp.bfloat16)
    normalized = lax.all_gather(normalized_local, "tp", axis=0, tiled=True)
    sequence_length = normalized.shape[0]
    heads_q = weight_q.shape[1] // HEAD_SIZE
    heads_kv = weight_k.shape[1] // HEAD_SIZE
    cosine_table, sine_table = rope_tables(sequence_length, HEAD_SIZE)
    query_rows = jnp.dot(normalized, weight_q, preferred_element_type=jnp.float32).reshape(
        sequence_length, heads_q, HEAD_SIZE
    )
    query_rows = rotate(query_rows, cosine_table, sine_table).astype(jnp.bfloat16)
    rotated_keys = jnp.dot(normalized, weight_k, preferred_element_type=jnp.float32).reshape(
        sequence_length, heads_kv, HEAD_SIZE
    )
    rotated_keys = rotate(rotated_keys, cosine_table, sine_table).astype(jnp.bfloat16)
    values_bfloat = (
        jnp.dot(normalized, weight_v, preferred_element_type=jnp.float32)
        .astype(jnp.bfloat16)
        .reshape(sequence_length, heads_kv, HEAD_SIZE)
    )
    replica_group = heads_q // heads_kv
    block_of_rows = min(512, sequence_length)
    query_input_gradient, key_input_gradient, value_input_gradient = attention_reverse(
        query_rows.reshape(sequence_length, heads_kv, replica_group, HEAD_SIZE),
        rotated_keys,
        values_bfloat,
        attention_gradient[0].reshape(sequence_length, heads_kv, replica_group, HEAD_SIZE),
        block_of_rows,
    )
    dquery = (
        reverse_rotation(
            query_input_gradient.reshape(sequence_length, heads_q, HEAD_SIZE),
            cosine_table,
            sine_table,
        )
        .astype(jnp.bfloat16)
        .reshape(sequence_length, heads_q * HEAD_SIZE)
    )
    key_gradient = (
        reverse_rotation(key_input_gradient, cosine_table, sine_table)
        .astype(jnp.bfloat16)
        .reshape(sequence_length, heads_kv * HEAD_SIZE)
    )
    value_gradient = value_input_gradient.astype(jnp.bfloat16).reshape(
        sequence_length, heads_kv * HEAD_SIZE
    )
    contract = (((0,), (0,)), ((), ()))
    grad_wq = lax.dot_general(
        normalized, dquery, contract, preferred_element_type=jnp.float32
    ).astype(jnp.bfloat16)
    grad_wk = lax.dot_general(
        normalized, key_gradient, contract, preferred_element_type=jnp.float32
    ).astype(jnp.bfloat16)
    grad_wv = lax.dot_general(
        normalized, value_gradient, contract, preferred_element_type=jnp.float32
    ).astype(jnp.bfloat16)
    back = (((1,), (1,)), ((), ()))
    partial_value = lax.dot_general(dquery, weight_q, back, preferred_element_type=jnp.float32)
    partial_value = partial_value + lax.dot_general(
        key_gradient, weight_k, back, preferred_element_type=jnp.float32
    )
    summed_rows = lax.psum_scatter(
        (
            partial_value
            + lax.dot_general(value_gradient, weight_v, back, preferred_element_type=jnp.float32)
        ).astype(jnp.bfloat16),
        "tp",
        scatter_dimension=0,
        tiled=True,
    ).astype(jnp.float32)
    gains_gradient = of_everyone(jnp.sum(summed_rows * normalized_input, axis=0), "tp")
    scaled_rows = summed_rows * norm_gains[None, :]
    gradient_rows = (
        inverse_norm
        * (
            scaled_rows
            - normalized_input * jnp.mean(scaled_rows * normalized_input, axis=-1, keepdims=True)
        )
    ).astype(jnp.bfloat16)
    delta = global_fragment - local_fragment[0].astype(jnp.float32)
    replicas = lax.axis_size("rep")
    delta_rows = sent_and_summed(delta, "rep", 0) / replicas
    row_count = delta_rows.shape[0]
    offset = lax.axis_index("rep") * row_count
    momentum_rows = lax.dynamic_slice_in_dim(momentum, offset, row_count, 0)
    global_rows = lax.dynamic_slice_in_dim(global_fragment, offset, row_count, 0)
    momentum_next = outer_momentum * momentum_rows + delta_rows
    global_next = global_rows - outer_rate * (delta_rows + outer_momentum * momentum_next)
    new_global, new_momentum = in_one_piece((global_next, momentum_next), "rep", 0, 1)
    return (
        grad_wq[None],
        grad_wk[None],
        grad_wv[None],
        gains_gradient[None],
        gradient_rows[None],
        new_global,
        new_momentum,
    )


def solution(mesh):
    placed = (
        P("rep", "tp", None),
        P("rep", None),
        P("rep", None, "tp"),
        P("rep", None, "tp"),
        P("rep", None, "tp"),
        P("rep", None, "tp"),
        P("tp", None),
        P("tp", None),
        P("rep", "tp", None),
    )
    return jax.shard_map(
        body,
        mesh=mesh,
        in_specs=placed,
        out_specs=(
            P("rep", None, "tp"),
            P("rep", None, "tp"),
            P("rep", None, "tp"),
            P("rep", None),
            P("rep", "tp", None),
            P("tp", None),
            P("tp", None),
        ),
        check_vma=False,
    )
```

profile of v0, /device:TPU:8, one launch (start us, length us, event | category | flops | bytes accessed | tf_op | source)
XLA Modules:
  0.0 287.1 jit_solution(629735918191153067)
XLA Ops:
  9.3 2.3 fusion.51
  14.2 11.3 %all-to-all-start.1 = ((f32[32,2,3072]{2,1,0:T(2,128)}), f32[32,2,3072]{2,1,0:T(2,128)S(1)}, u32[]{:S(2)}, u32[]{:S(2)}) async-start(f32[32,2,3072]{2,1,0:T(2,128)} %reshape.228), calls=%async_computation.2 | async-start | bytes 1572864 | tf_op jit(solution)/shard_map/all_to_all | solution.py:32
  30.3 20.0 %all-to-all-done.1 = f32[32,2,3072]{2,1,0:T(2,128)S(1)} async-done(((f32[32,2,3072]{2,1,0:T(2,128)}), f32[32,2,3072]{2,1,0:T(2,128)S(1)}, u32[]{:S(2)}, u32[]{:S(2)}) %all-to-all-start.1) | async-done | bytes 786464 | tf_op jit(solution)/shard_map/all_to_all | solution.py:32
  52.3 40.9 %all-gather.4.cloned.1.call-done = bf16[1024,3072]{1,0:T(8,128)(2,1)} async-done(((bf16[128,3072]{1,0:T(8,128)(2,1)}), bf16[1024,3072]{1,0:T(8,128)(2,1)}) %all-gather.4.cloned.1.call-update) | async-done | bytes 6291472 | tf_op jit(solution)/shard_map/all_gather | solution.py:138
  93.2 5.2 %fusion.39 = f32[1024,2,128]{0,2,1:T(8,128)S(1)} fusion(bf16[2,128,3072]{2,1,0:T(8,128)(2,1)} %bitcast.242, bf16[1024,3072]{1,0:T(8,128)(2,1)} %all-gather.4.cloned.1.call-done), kind=kOutput, calls=%fused_computation.43 | convolution fusion | flops 1610612736 | bytes 8912896 | tf_op jit(solution)/shard_map/dot_general | solution.py:143
  99.2 2.2 fusion.67
  101.5 2.9 %fusion.81 = (bf16[1024,1,128]{0,2,1:T(8,128)(2,1)}, f32[1024,128]{0,1:T(8,128)S(1)}, f32[1024,128]{0,1:T(8,128)S(1)}) fusion(f32[1024,64]{0,1:T(8,128)S(1)} %get-tuple-element.171, f32[1024,64]{0,1:T(8,128)S(1)} %get-tuple-element.170, f32[1024,128]{0,1:T(8,128)S(1)} %fusion.67, f32[1024,64]{0,1:T(8,128)S(1)} %copy-done.15), kind=kLoop, calls=%fused_computation.102 | loop fusion | flops 786432 | bytes 2621440 | tf_op jit(solution)/shard_map/convert_element_type | solution.py:150
  108.6 5.5 %fusion.57 = bf16[1024,1,128]{2,0,1:T(8,128)(2,1)} fusion(bf16[1024,3072]{1,0:T(8,128)(2,1)} %all-gather.4.cloned.1.call-done, bf16[1,3072,128]{2,1,0:T(8,128)(2,1)} %param.15), kind=kOutput, calls=%fused_computation.68 | convolution fusion | flops 805437440 | bytes 7340032 | tf_op jit(solution)/shard_map/dot_general | solution.py:152
  114.0 38.9 %while.15 = (s32[]{:T(128)}, f32[1024,1,128]{0,2,1:T(8,128)}, f32[1024,1,128]{0,2,1:T(8,128)}, f32[2,512,1,2,128]{4,1,3,2,0:T(8,128)}, s32[2]{0:T(128)S(1)}, /*i...) while((s32[]{:T(128)}, f32[1024,1,128]{0,2,1:T(8,128)}, ...), condition=%wide.region_5.6_spmd.clone, body=%wide.region_1.5_spmd.clone.sunk | while | flops 1370486272 | bytes 68469048 | solution.py:110
  118.9 3.3 %fusion.123 = (f32[2,512]{1,0:T(2,128)S(1)}, f32[512,2,1024]{2,0,1:T(8,128)S(1)}) fusion(f32[2,512]{1,0:T(2,128)S(1)} %fusion.122, f32[2,512]{1,0:T(2,128)S(1)} %get-tuple-element.237, f32[512,2,1024]{2,0,1:T(8,128)S(1)} %get-tuple-element.236, pred[512,1024]{1,0:T(8,128)(4,1)S(1)} %iota_compare_fusion.2, ...), kind=kOutput, calls=%fused_computation.3.clone.1 | convolution fusion | flops 274725888 | bytes 9449476 | tf_op jit(solution)/shard_map/while/body/eval_jaxpr/qgrd,kgd->grqk/dot_general | solution.py:92
  123.8 2.2 fusion.125
  126.0 4.6 %fusion.126 = f32[1024,1,128]{0,2,1:T(8,128)} fusion(f32[512,2,1024]{2,0,1:T(8,128)} %copy-done.1, f32[2,512]{1,0:T(2,128)S(1)} %fusion.122, f32[2,512]{1,0:T(2,128)S(1)} %get-tuple-element.237, pred[512,1024]{1,0:T(8,128)(4,1)S(1)} %iota_compare_fusion.2, f32[1024,1,128]{0,2,1:T(8,128)} %get-tuple-element.255, pred[]{:T(512)S(6)} %compare.3, ...), kind=kOutput, calls=%fused_computation.21.clone.1 | convolution fusion | flops 273940480 | bytes 6037509 | tf_op jit(solution)/shard_map/while/body/eval_jaxpr/grqk,qgrd->kgd/dot_general | solution.py:89
  138.2 3.3 %fusion.123 = (f32[2,512]{1,0:T(2,128)S(1)}, f32[512,2,1024]{2,0,1:T(8,128)S(1)}) fusion(f32[2,512]{1,0:T(2,128)S(1)} %fusion.122, f32[2,512]{1,0:T(2,128)S(1)} %get-tuple-element.237, f32[512,2,1024]{2,0,1:T(8,128)S(1)} %get-tuple-element.236, pred[512,1024]{1,0:T(8,128)(4,1)S(1)} %iota_compare_fusion.2, ...), kind=kOutput, calls=%fused_computation.3.clone.1 | convolution fusion | flops 274725888 | bytes 9449476 | tf_op jit(solution)/shard_map/while/body/eval_jaxpr/qgrd,kgd->grqk/dot_general | solution.py:92
  143.1 2.4 fusion.125
  145.5 4.8 %fusion.126 = f32[1024,1,128]{0,2,1:T(8,128)} fusion(f32[512,2,1024]{2,0,1:T(8,128)} %copy-done.1, f32[2,512]{1,0:T(2,128)S(1)} %fusion.122, f32[2,512]{1,0:T(2,128)S(1)} %get-tuple-element.237, pred[512,1024]{1,0:T(8,128)(4,1)S(1)} %iota_compare_fusion.2, f32[1024,1,128]{0,2,1:T(8,128)} %get-tuple-element.255, pred[]{:T(512)S(6)} %compare.3, ...), kind=kOutput, calls=%fused_computation.21.clone.1 | convolution fusion | flops 273940480 | bytes 6037509 | tf_op jit(solution)/shard_map/while/body/eval_jaxpr/grqk,qgrd->kgd/dot_general | solution.py:89
  152.9 2.3 copy.64
  157.6 2.7 fusion.80
  160.3 2.9 %fusion.79 = bf16[1024,1,128]{0,2,1:T(8,128)(2,1)S(1)} fusion(f32[1024,1,128]{0,2,1:T(8,128)S(1)} %copy-done.3, f32[1024,1,64]{0,2,1:T(8,128)} %get-tuple-element.175, f32[1024,1,64]{0,2,1:T(8,128)S(1)} %get-tuple-element.169, f32[1024,1,64]{0,2,1:T(8,128)S(1)} %get-tuple-element.168), kind=kLoop, calls=%fused_computation.99 | loop fusion | flops 655360 | bytes 1572864 | tf_op jit(solution)/shard_map/convert_element_type | solution.py:176
  164.6 6.4 %fusion.65 = f32[1024,3072]{1,0:T(8,128)} fusion(bf16[1,3072,128]{2,1,0:T(8,128)(2,1)S(1)} %copy-done, bf16[1024,1,128]{0,2,1:T(8,128)(2,1)S(1)} %fusion.79), kind=kOutput, calls=%fused_computation.81 | convolution fusion | flops 805306368 | bytes 13631488 | tf_op jit(solution)/shard_map/dot_general | solution.py:194
  171.0 6.4 %fusion.55 = f32[1024,3072]{1,0:T(8,128)} fusion(bf16[1024,256]{0,1:T(8,128)(2,1)S(1)} %bitcast.241, bf16[1,3072,256]{2,1,0:T(8,128)(2,1)S(1)} %copy-done.7), kind=kOutput, calls=%fused_computation.65 | convolution fusion | flops 1610612736 | bytes 14680064 | tf_op jit(solution)/shard_map/dot_general | solution.py:193
  177.4 12.0 %add_convert_fusion = bf16[1024,3072]{1,0:T(8,128)(2,1)} fusion(f32[1024,3072]{1,0:T(8,128)} %fusion.55, f32[1024,3072]{1,0:T(8,128)} %fusion.65, bf16[1,3072,128]{2,1,0:T(8,128)(2,1)S(1)} %copy-done.19, f32[1024,1,128]{0,2,1:T(8,128)S(1)} %copy-done.12), kind=kOutput, calls=%fused_computation.42 | convolution fusion | flops 814874624 | bytes 32768000 | tf_op jit(solution)/shard_map/dot_general | solution.py:200
  189.5 2.4 reshape.232
  193.1 3.0 %copy.62 = f32[2,512,1,2,128]{4,3,1,0,2:T(2,128)} copy(f32[2,512,1,2,128]{4,1,3,2,0:T(8,128)} %get-tuple-element.56) | data formatting | bytes 2097152 | tf_op jit(solution)/shard_map/while | solution.py:110
  196.2 2.7 copy.65
  200.0 2.5 copy.63
  202.5 6.3 %fusion.42 = bf16[1,3072,128]{2,1,0:T(8,128)(2,1)} fusion(bf16[1024,3072]{1,0:T(8,128)(2,1)} %all-gather.4.cloned.1.call-done, bf16[1024,1,128]{0,2,1:T(8,128)(2,1)} %copy-done.14), kind=kOutput, calls=%fused_computation.49 | convolution fusion | flops 805699584 | bytes 7340032 | tf_op jit(solution)/shard_map/dot_general | solution.py:186
  208.9 2.8 fusion.43
  211.6 3.1 %fusion.41 = bf16[1,3072,256]{2,1,0:T(8,128)(2,1)} fusion(bf16[1024,3072]{1,0:T(8,128)(2,1)S(1)} %bitcast.236, f32[1024,256]{1,0:T(8,128)S(1)} %copy-done.17, f32[1024,256]{1,0:T(8,128)S(1)} %copy-done.18, f32[128,8,2,128]{3,2,1,0:T(2,128)S(1)} %bitcast.243), kind=kOutput, calls=%fused_computation.46 | convolution fusion | flops 1612185600 | bytes 11010048 | tf_op jit(solution)/shard_map/dot_general | solution.py:183
  214.7 51.5 %reduce-scatter.2.cloned.1.call-done = bf16[128,3072]{1,0:T(8,128)(2,1)} async-done(((bf16[1024,3072]{1,0:T(8,128)(2,1)}), bf16[128,3072]{1,0:T(8,128)(2,1)}) %reduce-scatter.2.cloned.1.call-update) | async-done | bytes 786448 | tf_op jit(solution)/shard_map/reduce_scatter | solution.py:197
  268.9 6.0 %all-to-all-start = ((f32[8,1,3072]{2,1,0:T(1,128)}), f32[8,1,3072]{2,1,0:T(1,128)S(1)}, u32[]{:S(2)}, u32[]{:S(2)}) async-start(f32[8,1,3072]{2,1,0:T(1,128)} %broadcast_in_dim.52), calls=%async_computation.1 | async-start | bytes 196608 | tf_op jit(solution)/shard_map/all_to_all | solution.py:17
  274.8 2.7 fusion.62
  277.5 2.3 all-to-all-done
  (108 shorter events, 42.8 us)
Async XLA Ops:
  7.2 92.1 %copy-start = (bf16[1,3072,128]{2,1,0:T(8,128)(2,1)S(1)}, bf16[1,3072,128]{2,1,0:T(8,128)(2,1)}, u32[]{:S(2)}) copy-start(bf16[1,3072,128]{2,1,0:T(8,128)(2,1)} %param.14) | copy-start | bytes 2359300
  7.2 18.5 %copy-start.6 = (bf16[1,3072,256]{2,1,0:T(8,128)(2,1)S(1)}, bf16[1,3072,256]{2,1,0:T(8,128)(2,1)}, u32[]{:S(2)}) copy-start(bf16[1,3072,256]{2,1,0:T(8,128)(2,1)} %param.13) | copy-start | bytes 4718596
  7.2 86.0 %all-gather.4.cloned.1.call-start = ((), (), s32[]{:S(2)}) async-start(), calls=%async_computation.3 | async-start | bytes 7077888 | tf_op jit(solution)/shard_map/all_gather | solution.py:138
  14.2 36.1 %all-to-all-start.1 = ((f32[32,2,3072]{2,1,0:T(2,128)}), f32[32,2,3072]{2,1,0:T(2,128)S(1)}, u32[]{:S(2)}, u32[]{:S(2)}) async-start(f32[32,2,3072]{2,1,0:T(2,128)} %reshape.228), calls=%async_computation.2 | async-start | bytes 1572864 | tf_op jit(solution)/shard_map/all_to_all | solution.py:32
  25.6 163.9 %all-gather.6.cloned.1.call-start = ((), (), s32[]{:S(2)}) async-start(), calls=%async_computation.5 | async-start | bytes 1622016 | tf_op jit(solution)/shard_map/all_gather | solution.py:38
  52.2 214.0 %reduce-scatter.2.cloned.1.call-start = ((), (), s32[]{:S(2)}) async-start(), calls=%async_computation.4 | async-start | bytes 7077888 | tf_op jit(solution)/shard_map/reduce_scatter | solution.py:197
  93.2 6.1 %copy-start.2 = (bf16[1024,3072]{1,0:T(8,128)(2,1)S(1)}, bf16[1024,3072]{1,0:T(8,128)(2,1)}, u32[]{:S(2)}) copy-start(bf16[1024,3072]{1,0:T(8,128)(2,1)} %all-gather.4.cloned.1.call-done) | copy-start | bytes 18874372
  99.2 2.3 copy-start.15
  104.4 9.6 %copy-start.4 = (f32[1024,128]{0,1:T(8,128)}, f32[1024,128]{0,1:T(8,128)S(1)}, u32[]{:S(2)}) copy-start(f32[1024,128]{0,1:T(8,128)S(1)} %get-tuple-element.174) | copy-start | bytes 1572868
  104.4 9.6 %copy-start.8 = (f32[1024,128]{0,1:T(8,128)}, f32[1024,128]{0,1:T(8,128)S(1)}, u32[]{:S(2)}) copy-start(f32[1024,128]{0,1:T(8,128)S(1)} %get-tuple-element.173) | copy-start | bytes 1572868
  117.7 4.5 %copy-start.1 = (f32[512,2,1024]{2,0,1:T(8,128)}, f32[512,2,1024]{2,0,1:T(8,128)S(1)}, u32[]{:S(2)}) copy-start(f32[512,2,1024]{2,0,1:T(8,128)S(1)} %get-tuple-element.236) | copy-start | bytes 12582916 | tf_op jit(solution)/shard_map/while
  126.0 4.6 %copy-start.10 = (f32[2,512,1,2,128]{4,1,3,2,0:T(8,128)S(1)}, f32[2,512,1,2,128]{4,1,3,2,0:T(8,128)}, u32[]{:S(2)}) copy-start(f32[2,512,1,2,128]{4,1,3,2,0:T(8,128)} %get-tuple-element.256) | copy-start | bytes 3145732 | tf_op jit(solution)/shard_map/while
  132.3 1.0 copy-start.11
  137.0 4.5 %copy-start.1 = (f32[512,2,1024]{2,0,1:T(8,128)}, f32[512,2,1024]{2,0,1:T(8,128)S(1)}, u32[]{:S(2)}) copy-start(f32[512,2,1024]{2,0,1:T(8,128)S(1)} %get-tuple-element.236) | copy-start | bytes 12582916 | tf_op jit(solution)/shard_map/while
  145.5 4.8 %copy-start.10 = (f32[2,512,1,2,128]{4,1,3,2,0:T(8,128)S(1)}, f32[2,512,1,2,128]{4,1,3,2,0:T(8,128)}, u32[]{:S(2)}) copy-start(f32[2,512,1,2,128]{4,1,3,2,0:T(8,128)} %get-tuple-element.256) | copy-start | bytes 3145732 | tf_op jit(solution)/shard_map/while
  151.9 1.0 copy-start.11
  152.9 4.5 %copy-start.9 = (f32[1024,128]{0,1:T(8,128)S(1)}, f32[1024,128]{0,1:T(8,128)}, u32[]{:S(2)}) copy-start(f32[1024,128]{0,1:T(8,128)} %copy-done.8) | copy-start | bytes 1572868
  152.9 4.6 %copy-start.3 = (f32[1024,1,128]{0,2,1:T(8,128)S(1)}, f32[1024,1,128]{0,2,1:T(8,128)}, u32[]{:S(2)}) copy-start(f32[1024,1,128]{0,2,1:T(8,128)} %get-tuple-element.57) | copy-start | bytes 1572868
  157.4 6.0 %copy-start.5 = (f32[1024,128]{0,1:T(8,128)S(1)}, f32[1024,128]{0,1:T(8,128)}, u32[]{:S(2)}) copy-start(f32[1024,128]{0,1:T(8,128)} %copy-done.4) | copy-start | bytes 1572868
  163.3 7.7 %copy-start.14 = (bf16[1024,1,128]{0,2,1:T(8,128)(2,1)}, bf16[1024,1,128]{0,2,1:T(8,128)(2,1)S(1)}, u32[]{:S(2)}) copy-start(bf16[1024,1,128]{0,2,1:T(8,128)(2,1)S(1)} %fusion.79) | copy-start | bytes 786436
  164.6 6.4 %copy-start.7 = (bf16[1,3072,256]{2,1,0:T(8,128)(2,1)S(1)}, bf16[1,3072,256]{2,1,0:T(8,128)(2,1)}, u32[]{:S(2)}) copy-start(bf16[1,3072,256]{2,1,0:T(8,128)(2,1)} %param.13) | copy-start | bytes 4718596
  171.0 6.4 %copy-start.12 = (f32[1024,1,128]{0,2,1:T(8,128)S(1)}, f32[1024,1,128]{0,2,1:T(8,128)}, u32[]{:S(2)}) copy-start(f32[1024,1,128]{0,2,1:T(8,128)} %get-tuple-element.58) | copy-start | bytes 1572868
  171.0 6.4 %copy-start.19 = (bf16[1,3072,128]{2,1,0:T(8,128)(2,1)S(1)}, bf16[1,3072,128]{2,1,0:T(8,128)(2,1)}, u32[]{:S(2)}) copy-start(bf16[1,3072,128]{2,1,0:T(8,128)(2,1)} %param.15) | copy-start | bytes 2359300
  196.2 12.6 %slice-start = ((s8[6291456]{0:T(1024)(128)(4,1)}), s8[2097152]{0:T(1024)(128)(4,1)S(1)}, s32[]{:S(2)}) async-start(s8[6291456]{0:T(1024)(128)(4,1)} %bitcast.235), calls=%async_computation.6 | async-start | bytes 4194304
  202.5 6.3 %slice-start.1 = ((s8[6291456]{0:T(1024)(128)(4,1)}), s8[4194304]{0:T(1024)(128)(4,1)S(1)}, s32[]{:S(2)}) async-start(s8[6291456]{0:T(1024)(128)(4,1)} %bitcast.235), calls=%async_computation.7 | async-start | bytes 8388608
  202.5 6.3 %copy-start.13 = (f32[1024,1,128]{0,2,1:T(8,128)S(1)}, f32[1024,1,128]{0,2,1:T(8,128)}, u32[]{:S(2)}) copy-start(f32[1024,1,128]{0,2,1:T(8,128)} %get-tuple-element.58) | copy-start | bytes 1572868
  208.8 2.8 copy-start.16
  208.8 2.8 copy-start.17
  208.9 2.8 copy-start.18
  211.6 54.6 %copy-start.20 = (f32[1,3072]{1,0:T(1,128)S(1)}, f32[1,3072]{1,0:T(1,128)}, u32[]{:S(2)}) copy-start(f32[1,3072]{1,0:T(1,128)} %param.12) | copy-start | bytes 36868
  211.6 54.6 %copy-start.22 = (f32[128]{0:T(128)S(1)}, f32[128]{0:T(128)}, u32[]{:S(2)}) copy-start(f32[128]{0:T(128)} %copy-done.21) | copy-start | bytes 1540
  268.9 11.0 %all-to-all-start = ((f32[8,1,3072]{2,1,0:T(1,128)}), f32[8,1,3072]{2,1,0:T(1,128)S(1)}, u32[]{:S(2)}, u32[]{:S(2)}) async-start(f32[8,1,3072]{2,1,0:T(1,128)} %broadcast_in_dim.52), calls=%async_computation.1 | async-start | bytes 196608 | tf_op jit(solution)/shard_map/all_to_all | solution.py:17
  (1 other events, 0.5 us)
Sparse Core Ops, SparseCore 0:
  11.7 81.4 all-gather.3
  95.9 81.8 all-gather.5
  189.6 76.6 reduce-scatter.1
where the time goes:
time: 289 us; the launch traced here: 287 us
  waiting for transfers between devices  115 us (40%)
  matrix products  77.9 us (27%)
  other arithmetic  32.6 us (11%)
  local copies, waits for them, and re-layouts  29.1 us (10%)
  starting transfers between devices  17.4 us (6%)
  between operations  14 us (5%)
    reduce_scatter x1, waiting for transfers between devices, body(): lax.psum_scatter((partial_value + lax.dot_general(value_gradient, weight_...  51.5 us
    all_gather x1, waiting for transfers between devices, body(): normalized = lax.all_gather(normalized_local, 'tp', axis=0, tiled=True)  40.9 us
    all_to_all x1, waiting for transfers between devices, sent_and_summed(): lax.all_to_all(parts, axis, split_axis=0, concat_axis=0, tiled=True)  20 us
    dot_general x1, matrix products, body(): lax.dot_general(value_gradient, weight_v, back, preferred_element_type=jn...  12 us
    all_to_all x1, starting transfers between devices, sent_and_summed(): lax.all_to_all(parts, axis, split_axis=0, concat_axis=0, tiled=True)  11.3 us
    dot_general x2, matrix products, one_block(): jnp.einsum('grqk,qgrd->kgd', prob_low, grad_block, preferred_element_type...  9.39 us
    unnamed x47, local copies, waits for them, and re-layouts  7 us
    dot_general x2, matrix products, one_block(): jnp.einsum('qgrd,kgd->grqk', grad_block, values_bfloat, preferred_element...  6.59 us
  transfers between devices with their start and end apart: 5, of which 4 were waited for; matrix products, arithmetic and copies ran while one was open for 45% of the time, Pallas kernels for 0%

commit v1 on v0

v1 whole, which is shorter than its diff:
```python
import jax
import jax.numpy as jnp
import numpy as np
from jax import lax
from jax.experimental import pallas as pl
from jax.experimental.pallas import tpu as pltpu
from jax.sharding import PartitionSpec as P

HEAD = 128
EPSILON = 1e-05
ROPE_BASE = 500000.0
OUTER_RATE = 0.7
OUTER_MOMENTUM = 0.9
NEGATIVE = -1e30


def rope_constants(seq):
    half = HEAD // 2
    freq = ROPE_BASE ** (-2.0 * np.arange(half, dtype=np.float64) / HEAD)
    angle = np.arange(seq, dtype=np.float64)[:, None] * freq[None, :]
    cos, sin = np.cos(angle), np.sin(angle)
    table = np.concatenate([cos, cos, -sin, sin], axis=1)
    return jnp.asarray(table.astype(np.float32))


def rope(v, cos, sin):
    return v * cos + pltpu.roll(v, HEAD // 2, 1) * sin


def unrope(g, cos, sin):
    return g * cos - pltpu.roll(g, HEAD // 2, 1) * sin


def project(rows, x, weights, table, qkv):
    heads = qkv.shape[1] // HEAD
    cos = table[rows, :HEAD]
    sin = table[rows, HEAD:]
    out = jnp.dot(x, weights[...], preferred_element_type=jnp.float32)
    for h in range(heads):
        part = out[:, h * HEAD : (h + 1) * HEAD]
        if h < heads - 1:
            part = rope(part, cos, sin)
        qkv[rows, h * HEAD : (h + 1) * HEAD] = part.astype(jnp.bfloat16)


def dot_t(a, b):
    return lax.dot_general(a, b, (((1,), (1,)), ((), ())), preferred_element_type=jnp.float32)


def t_dot(a, b):
    return lax.dot_general(a, b, (((0,), (0,)), ((), ())), preferred_element_type=jnp.float32)


def attention_rows(start, block, qkv, dout, table, dqkv, acc_k, acc_v, first):
    width = start + block
    scale = HEAD ** (-0.5)
    heads = dout.shape[1] // HEAD
    at_k, at_v = heads * HEAD, (heads + 1) * HEAD
    keys = qkv[:width, at_k : at_k + HEAD]
    values = qkv[:width, at_v : at_v + HEAD]
    rows = slice(start, start + block)
    row = lax.broadcasted_iota(jnp.int32, (block, block), 0)
    col = lax.broadcasted_iota(jnp.int32, (block, block), 1)
    allowed = col <= row
    cos, sin = table[rows, :HEAD], table[rows, HEAD:]
    dk = dv = None
    for h in range(heads):
        q = qkv[rows, h * HEAD : (h + 1) * HEAD]
        do = dout[rows, h * HEAD : (h + 1) * HEAD]
        s = dot_t(q, keys)
        last = jnp.where(allowed, s[:, start:], NEGATIVE)
        s = last if start == 0 else jnp.concatenate([s[:, :start], last], axis=1)
        top = jnp.max(s, axis=1, keepdims=True)
        power = jnp.exp((s - top) * scale)
        p = power * (1.0 / jnp.sum(power, axis=1, keepdims=True))
        dp = dot_t(do, values)
        drop = jnp.sum(dp * p, axis=1, keepdims=True)
        ds = ((p * (dp - drop)) * scale).astype(jnp.bfloat16)
        p_low = p.astype(jnp.bfloat16)
        dq = jnp.dot(ds, keys, preferred_element_type=jnp.float32)
        dqkv[rows, h * HEAD : (h + 1) * HEAD] = unrope(dq, cos, sin).astype(jnp.bfloat16)
        tv, tk = t_dot(p_low, do), t_dot(ds, q)
        dv = tv if dv is None else dv + tv
        dk = tk if dk is None else dk + tk
    if first:
        acc_v[:width, :] = dv
        acc_k[:width, :] = dk
    else:
        acc_v[:width, :] += dv
        acc_k[:width, :] += dk
    width = start
    heads_at = heads * HEAD
    dqkv[rows, heads_at : heads_at + HEAD] = unrope(acc_k[rows, :], cos, sin).astype(jnp.bfloat16)
    dqkv[rows, heads_at + HEAD : heads_at + 2 * HEAD] = acc_v[rows, :].astype(jnp.bfloat16)


def attention(block, qkv, dout, table, dqkv, acc_k, acc_v):
    seq = qkv.shape[0]
    for start in reversed(range(0, seq, block)):
        attention_rows(start, block, qkv, dout, table, dqkv, acc_k, acc_v, start + block == seq)


def weight_grads(x, dqkv, block, outs):
    depth = x.shape[1]

    def one(j, carry):
        at = pl.multiple_of(j * block, block)
        g = t_dot(x[:, pl.ds(at, block)], dqkv[...]).astype(jnp.bfloat16)
        done = 0
        for o in outs:
            o[pl.ds(at, block), :] = g[:, done : done + o.shape[1]]
            done += o.shape[1]
        return carry

    lax.fori_loop(0, depth // block, one, 0)


def local_kernel(x, wq, wk, wv, dout, table, part, gq, gk, gv, weights, qkv, dqkv, acc_k, acc_v):
    seq, depth = x.shape
    weights[:, : wq.shape[1]] = wq[...]
    weights[:, wq.shape[1] : wq.shape[1] + HEAD] = wk[...]
    weights[:, wq.shape[1] + HEAD :] = wv[...]
    rows = 256

    def proj(i, carry):
        r = pl.ds(pl.multiple_of(i * rows, rows), rows)
        project(r, x[r, :], weights, table, qkv)
        return carry

    lax.fori_loop(0, seq // rows, proj, 0)
    attention(256, qkv, dout, table, dqkv, acc_k, acc_v)

    def back(i, carry):
        r = pl.ds(pl.multiple_of(i * rows, rows), rows)
        part[r, :] = dot_t(dqkv[r, :], weights[...]).astype(jnp.bfloat16)
        return carry

    lax.fori_loop(0, seq // rows, back, 0)
    weight_grads(x, dqkv, 256, (gq, gk, gv))


def local(x, wq, wk, wv, dout):
    seq, depth = x.shape
    table = rope_constants(seq)
    bf = jnp.bfloat16
    cols = wq.shape[1] + wk.shape[1] + wv.shape[1]
    vm = pl.BlockSpec(memory_space=pltpu.VMEM)
    return pl.pallas_call(
        local_kernel,
        out_shape=(
            jax.ShapeDtypeStruct((seq, depth), bf),
            jax.ShapeDtypeStruct(wq.shape, bf),
            jax.ShapeDtypeStruct(wk.shape, bf),
            jax.ShapeDtypeStruct(wv.shape, bf),
        ),
        in_specs=[vm] * 6,
        out_specs=[vm] * 4,
        scratch_shapes=[
            pltpu.VMEM((depth, cols), bf),
            pltpu.VMEM((seq, cols), bf),
            pltpu.VMEM((seq, cols), bf),
            pltpu.VMEM((seq, HEAD), jnp.float32),
            pltpu.VMEM((seq, HEAD), jnp.float32),
        ],
        compiler_params=pltpu.CompilerParams(vmem_limit_bytes=60 * 1024 * 1024),
        cost_estimate=pl.CostEstimate(
            flops=2 * seq * cols * depth * 3, bytes_accessed=20_000_000, transcendentals=0
        ),
    )(x, wq, wk, wv, dout, table)


def body(tokens, norm_gain, w_query, key_weight, value_weight, attention_gradient, global_fragment, momentum, local_fragment):
    gain = norm_gain[0]
    wide = tokens[0].astype(jnp.float32)
    inverse = lax.rsqrt(jnp.mean(wide * wide, axis=-1, keepdims=True) + EPSILON)
    xhat = wide * inverse
    normed = lax.all_gather((xhat * gain[None, :]).astype(jnp.bfloat16), "tp", axis=0, tiled=True)
    part, gq, gk, gv = local(normed, w_query[0], key_weight[0], value_weight[0], attention_gradient[0])
    summed = lax.psum_scatter(part, "tp", scatter_dimension=0, tiled=True).astype(jnp.float32)
    own = jnp.sum(summed * xhat, axis=0)
    grad_gain = jnp.sum(lax.all_gather(own, "tp", axis=0), axis=0)
    scaled = summed * gain[None, :]
    grad_tokens = (inverse * (scaled - xhat * jnp.mean(scaled * xhat, axis=-1, keepdims=True))).astype(jnp.bfloat16)
    replicas = lax.axis_size("rep")
    rows = global_fragment.shape[0] // replicas
    mine = local_fragment[0].reshape(replicas, rows, -1)
    arrived = lax.all_to_all(mine, "rep", split_axis=0, concat_axis=0, tiled=True)
    at = lax.axis_index("rep") * rows
    globals_ = lax.dynamic_slice_in_dim(global_fragment, at, rows, 0)
    mean_rows = globals_ - jnp.sum(arrived.astype(jnp.float32), axis=0) / replicas
    mean = lax.all_gather(mean_rows, "rep", axis=0, tiled=True)
    new_momentum = OUTER_MOMENTUM * momentum + mean
    new_global = global_fragment - OUTER_RATE * (mean + OUTER_MOMENTUM * new_momentum)
    return (gq[None], gk[None], gv[None], grad_gain[None], grad_tokens[None], new_global, new_momentum)


def solution(mesh):
    placed = (
        P("rep", "tp", None), P("rep", None), P("rep", None, "tp"), P("rep", None, "tp"), P("rep", None, "tp"),
        P("rep", None, "tp"), P("tp", None), P("tp", None), P("rep", "tp", None),
    )
    outs = (P("rep", None, "tp"), P("rep", None, "tp"), P("rep", None, "tp"), P("rep", None), P("rep", "tp", None), P("tp", None), P("tp", None))
    return jax.shard_map(body, mesh=mesh, in_specs=placed, out_specs=outs, check_vma=False)
```

time: 289 us -> 239 us (0.83)
  matrix products: 77.9 us -> 0 us
  blocking collectives: 0 us -> 69.4 us
  Pallas kernels: 0 us -> 28.6 us
  local copies, waits for them, and re-layouts: 29.1 us -> 2.45 us
  other arithmetic: 32.6 us -> 9.07 us
  waiting for transfers between devices: 115 us -> 102 us
  starting transfers between devices: 17.4 us -> 9.89 us
    dot_general x19 -> x0, matrix products: 77.9 us -> none  [the longest x1 12 us: body(): lax.dot_general(value_gradient, weight_v, back, preferred_element_type=jn...]
    all_gather x0 -> x2, blocking collectives: none -> 69.4 us  [the longest x1 39.4 us: body(): mean = lax.all_gather(mean_rows, 'rep', axis=0, tiled=True)]
    reduce_scatter x1, waiting for transfers between devices: 51.5 us -> 9.21 us  [body(): lax.psum_scatter(part, 'tp', scatter_dimension=0, tiled=True)]
    all_gather x2 -> x1, waiting for transfers between devices: 40.9 us -> 75.5 us  [body(): lax.all_gather((xhat * gain[None, :]).astype(jnp.bfloat16), 'tp', axis=0,...]
    pallas_call x0 -> x1, Pallas kernels: none -> 28.6 us  [local(): pl.pallas_call(local_kernel, out_shape=(jax.ShapeDtypeStruct((seq, depth)...]
    all_to_all x2 -> x1, starting transfers between devices: 17.3 us -> 9.81 us  [body(): lax.all_to_all(mine, 'rep', split_axis=0, concat_axis=0, tiled=True)]
    while x14 -> x0, local copies, waits for them, and re-layouts: 7.44 us -> none  [the longest x2 5.39 us: attention_reverse(): lax.scan(one_block, (initial, initial), jnp.arange(sequence_length // blo...]
    convert_element_type x4 -> x1, other arithmetic: 9.34 us -> 2.28 us  [body(): (xhat * gain[None, :]).astype(jnp.bfloat16)]
  transfers between devices with their start and end apart: 5 -> 3, of which waited for: 4 -> 3; matrix products, arithmetic and copies ran while one was open for 45% -> 1% of each run, Pallas kernels for 0% -> 0%
where the time goes in v1:
time: 239 us; the launch traced here: 236 us
  waiting for transfers between devices  102 us (43%)
  blocking collectives  69.4 us (29%)
  Pallas kernels  28.6 us (12%)
  between operations  14.1 us (6%)
  starting transfers between devices  9.89 us (4%)
  other arithmetic  9.07 us (4%)
  local copies, waits for them, and re-layouts  2.45 us (1%)
    all_gather x1, waiting for transfers between devices, body(): lax.all_gather((xhat * gain[None, :]).astype(jnp.bfloat16), 'tp', axis=0,...  75.5 us
    all_gather x1, blocking collectives, body(): mean = lax.all_gather(mean_rows, 'rep', axis=0, tiled=True)  39.4 us
    all_gather x1, blocking collectives, body(): grad_gain = jnp.sum(lax.all_gather(own, 'tp', axis=0), axis=0)  30 us
    pallas_call x1, Pallas kernels, local(): pl.pallas_call(local_kernel, out_shape=(jax.ShapeDtypeStruct((seq, depth)...  28.6 us
    all_to_all x1, waiting for transfers between devices, body(): lax.all_to_all(mine, 'rep', split_axis=0, concat_axis=0, tiled=True)  17.3 us
    all_to_all x1, starting transfers between devices, body(): lax.all_to_all(mine, 'rep', split_axis=0, concat_axis=0, tiled=True)  9.81 us
    reduce_scatter x1, waiting for transfers between devices, body(): lax.psum_scatter(part, 'tp', scatter_dimension=0, tiled=True)  9.21 us
  transfers between devices with their start and end apart: 3, of which 3 were waited for; matrix products, arithmetic and copies ran while one was open for 1% of the time, Pallas kernels for 0%

profile of v1, /device:TPU:8, one launch (start us, length us, event | category | flops | bytes accessed | tf_op | source)
XLA Modules:
  0.0 235.6 jit_solution(1306110105125629367)
XLA Ops:
  7.2 0.0 all-gather.4.cloned.1.call-start
  7.2 1.4 fusion.10
  8.6 2.3 fusion.7
  10.9 0.0 all-gather.4.cloned.1.call-update
  10.9 0.0 reduce-scatter.2.cloned.1.call-start
  11.0 75.5 %all-gather.4.cloned.1.call-done.x = bf16[1024,3072]{1,0:T(8,128)(2,1)} async-done(((bf16[128,3072]{1,0:T(8,128)(2,1)}), bf16[1024,3072]{1,0:T(8,128)(2,1)}) %all-gather.4.cloned.1.call-update) | async-done | bytes 6291472 | tf_op jit(solution)/shard_map/all_gather | solution.py:177
  86.5 28.6 %shard_map.153 = (bf16[1024,3072]{1,0:T(8,128)(2,1)}, bf16[3072,256]{1,0:T(8,128)(2,1)}, bf16[3072,128]{1,0:T(8,128)(2,1)}, bf16[3072,128]{1,0:T(8,128)(2,1)}) custom-call(bf16[1024,3072]{1,0:T(8,128)(2,1)} %all-gather.4.cloned.1.call-done.x, bf16[3072,256]{1,0:T(8,128)(2,1)} %bitcast.24, bf16[3072,128]{1,0:T(8,128)(2,1)} %bitcast.25, ...), custom_call_target="tpu_custom_call" | custom-call | flops 9663676416 | bytes 20000000 | tf_op jit(solution)/shard_map/pallas_call | solution.py:148
  115.1 0.0 copy-start.4
  115.1 0.0 reduce-scatter.2.cloned.1.call-update
  115.1 1.0 copy-done.4
  116.1 0.0 copy-start.2
  116.1 0.9 reshape_squeeze.3
  117.0 9.8 %all-to-all-start = ((bf16[32,2,3072]{2,1,0:T(2,128)(2,1)}), bf16[32,2,3072]{2,1,0:T(2,128)(2,1)S(1)}, u32[]{:S(2)}, u32[]{:S(2)}) async-start(bf16[32,2,3072]{2,1,0:T(2,128)(2,1)} %reshape_squeeze.3), calls=%async_computation.1 | async-start | bytes 786432 | tf_op jit(solution)/shard_map/all_to_all | solution.py:187
  126.8 0.0 copy-start.3
  126.8 17.3 %all-to-all-done = bf16[32,2,3072]{2,1,0:T(2,128)(2,1)S(1)} async-done(((bf16[32,2,3072]{2,1,0:T(2,128)(2,1)}), bf16[32,2,3072]{2,1,0:T(2,128)(2,1)S(1)}, u32[]{:S(2)}, u32[]{:S(2)}) %all-to-all-start) | async-done | bytes 393248 | tf_op jit(solution)/shard_map/all_to_all | solution.py:187
  144.1 0.3 convert_reduce_fusion
  144.5 0.0 copy-done.2
  144.5 39.4 %all-gather.1 = f32[32,2,3072]{2,1,0:T(2,128)S(1)} all-gather(f32[1,2,3072]{2,1,0:T(2,128)S(1)} %subtract_bitcast_fusion), channel_id=1, replica_groups=mesh['rep'=32,'tp'=8] {'rep'}, dimensions={0}, use_global_device_ids=true | all-gather | bytes 811008 | tf_op jit(solution)/shard_map/all_gather | solution.py:191
  183.9 0.5 reshape.31
  184.4 0.0 copy-done.3
  184.4 0.0 copy-start
  184.4 0.0 copy-start.5
  184.4 1.3 multiply_subtract_fusion
  185.8 9.2 %reduce-scatter.2.cloned.1.call-done = bf16[128,3072]{1,0:T(8,128)(2,1)} async-done(((bf16[1024,3072]{1,0:T(8,128)(2,1)}), bf16[128,3072]{1,0:T(8,128)(2,1)}) %reduce-scatter.2.cloned.1.call-update) | async-done | bytes 786448 | tf_op jit(solution)/shard_map/reduce_scatter | solution.py:179
  195.0 0.0 copy-done
  195.0 0.0 copy-done.5
  195.0 0.0 copy-start.1
  195.0 1.8 fusion.9
  196.8 30.0 %all-gather = f32[24576]{0:T(1024)S(1)} all-gather(f32[3072]{0:T(1024)S(1)} %get-tuple-element.16), channel_id=2, replica_groups=mesh['rep'=32,'tp'=8] {'tp'}, dimensions={0}, use_global_device_ids=true | all-gather | bytes 110592 | tf_op jit(solution)/shard_map/all_gather | solution.py:181
  226.8 0.6 reduce_sum.47
  227.5 0.0 copy-done.1
  227.5 1.3 fusion.11
  (4 shorter events, 0.1 us)
Async XLA Ops:
  7.2 79.3 %all-gather.4.cloned.1.call-start = ((), (), s32[]{:S(2)}) async-start(), calls=%async_computation.2 | async-start | bytes 7077888 | tf_op jit(solution)/shard_map/all_gather | solution.py:177
  10.9 184.1 %reduce-scatter.2.cloned.1.call-start = ((), (), s32[]{:S(2)}) async-start(), calls=%async_computation.3 | async-start | bytes 7077888 | tf_op jit(solution)/shard_map/reduce_scatter | solution.py:179
  115.1 1.0 copy-start.4
  116.1 28.4 %copy-start.2 = (f32[64,3072]{1,0:T(8,128)S(1)}, f32[64,3072]{1,0:T(8,128)}, u32[]{:S(2)}) copy-start(f32[64,3072]{1,0:T(8,128)} %param.16) | copy-start | bytes 2359300
  117.0 27.2 %all-to-all-start = ((bf16[32,2,3072]{2,1,0:T(2,128)(2,1)}), bf16[32,2,3072]{2,1,0:T(2,128)(2,1)S(1)}, u32[]{:S(2)}, u32[]{:S(2)}) async-start(bf16[32,2,3072]{2,1,0:T(2,128)(2,1)} %reshape_squeeze.3), calls=%async_computation.1 | async-start | bytes 786432 | tf_op jit(solution)/shard_map/all_to_all | solution.py:187
  126.8 57.6 %copy-start.3 = (f32[64,3072]{1,0:T(8,128)S(1)}, f32[64,3072]{1,0:T(8,128)}, u32[]{:S(2)}) copy-start(f32[64,3072]{1,0:T(8,128)} %param.17) | copy-start | bytes 2359300
  184.4 10.6 %copy-start = (bf16[1,128,3072]{2,1,0:T(8,128)(2,1)S(1)}, bf16[1,128,3072]{2,1,0:T(8,128)(2,1)}, u32[]{:S(2)}) copy-start(bf16[1,128,3072]{2,1,0:T(8,128)(2,1)} %param.10) | copy-start | bytes 2359300
  184.4 10.6 %copy-start.5 = (f32[1,3072]{1,0:T(1,128)S(1)}, f32[1,3072]{1,0:T(1,128)}, u32[]{:S(2)}) copy-start(f32[1,3072]{1,0:T(1,128)} %param.11) | copy-start | bytes 36868
  195.0 32.5 %copy-start.1 = (bf16[128,3072]{1,0:T(8,128)(2,1)S(1)}, bf16[128,3072]{1,0:T(8,128)(2,1)}, u32[]{:S(2)}) copy-start(bf16[128,3072]{1,0:T(8,128)(2,1)} %reduce-scatter.2.cloned.1.call-done) | copy-start | bytes 2359300
Sparse Core Ops, SparseCore 0:
  11.0 75.4 all-gather.3
  115.2 79.7 reduce-scatter.1

commit v2 on v1

v2 whole, which is shorter than its diff:
```python
import functools

import jax
import jax.numpy as jnp
import numpy as np
from jax import lax
from jax.experimental import pallas as pl
from jax.experimental.pallas import tpu as pltpu
from jax.sharding import PartitionSpec as P

HEAD = 128
EPSILON = 1e-05
ROPE_BASE = 500000.0
OUTER_RATE = 0.7
OUTER_MOMENTUM = 0.9
NEGATIVE = -1e30


def rope_constants(seq):
    half = HEAD // 2
    freq = ROPE_BASE ** (-2.0 * np.arange(half, dtype=np.float64) / HEAD)
    angle = np.arange(seq, dtype=np.float64)[:, None] * freq[None, :]
    cos, sin = np.cos(angle), np.sin(angle)
    table = np.concatenate([cos, cos, -sin, sin], axis=1)
    return jnp.asarray(table.astype(np.float32))


def rope(v, cos, sin):
    return v * cos + pltpu.roll(v, HEAD // 2, 1) * sin


def unrope(g, cos, sin):
    return g * cos - pltpu.roll(g, HEAD // 2, 1) * sin


def project(rows, x, weights, table, qkv):
    heads = qkv.shape[1] // HEAD
    cos = table[rows, :HEAD]
    sin = table[rows, HEAD:]
    out = jnp.dot(x, weights[...], preferred_element_type=jnp.float32)
    for h in range(heads):
        part = out[:, h * HEAD : (h + 1) * HEAD]
        if h < heads - 1:
            part = rope(part, cos, sin)
        qkv[rows, h * HEAD : (h + 1) * HEAD] = part.astype(jnp.bfloat16)


def dot_t(a, b):
    return lax.dot_general(a, b, (((1,), (1,)), ((), ())), preferred_element_type=jnp.float32)


def t_dot(a, b):
    return lax.dot_general(a, b, (((0,), (0,)), ((), ())), preferred_element_type=jnp.float32)


def attention_rows(start, block, qkv, dout, table, dqkv, acc_k, acc_v, first):
    width = start + block
    scale = HEAD ** (-0.5)
    heads = dout.shape[1] // HEAD
    at_k, at_v = heads * HEAD, (heads + 1) * HEAD
    keys = qkv[:width, at_k : at_k + HEAD]
    values = qkv[:width, at_v : at_v + HEAD]
    rows = slice(start, start + block)
    row = lax.broadcasted_iota(jnp.int32, (block, block), 0)
    col = lax.broadcasted_iota(jnp.int32, (block, block), 1)
    allowed = col <= row
    cos, sin = table[rows, :HEAD], table[rows, HEAD:]
    dk = dv = None
    for h in range(heads):
        q = qkv[rows, h * HEAD : (h + 1) * HEAD]
        do = dout[rows, h * HEAD : (h + 1) * HEAD]
        s = dot_t(q, keys)
        last = jnp.where(allowed, s[:, start:], NEGATIVE)
        s = last if start == 0 else jnp.concatenate([s[:, :start], last], axis=1)
        top = jnp.max(s, axis=1, keepdims=True)
        power = jnp.exp((s - top) * scale)
        p = power * (1.0 / jnp.sum(power, axis=1, keepdims=True))
        dp = dot_t(do, values)
        drop = jnp.sum(dp * p, axis=1, keepdims=True)
        ds = ((p * (dp - drop)) * scale).astype(jnp.bfloat16)
        p_low = p.astype(jnp.bfloat16)
        dq = jnp.dot(ds, keys, preferred_element_type=jnp.float32)
        dqkv[rows, h * HEAD : (h + 1) * HEAD] = unrope(dq, cos, sin).astype(jnp.bfloat16)
        tv, tk = t_dot(p_low, do), t_dot(ds, q)
        dv = tv if dv is None else dv + tv
        dk = tk if dk is None else dk + tk
    if first:
        acc_v[:width, :] = dv
        acc_k[:width, :] = dk
    else:
        acc_v[:width, :] += dv
        acc_k[:width, :] += dk
    width = start
    heads_at = heads * HEAD
    dqkv[rows, heads_at : heads_at + HEAD] = unrope(acc_k[rows, :], cos, sin).astype(jnp.bfloat16)
    dqkv[rows, heads_at + HEAD : heads_at + 2 * HEAD] = acc_v[rows, :].astype(jnp.bfloat16)


def attention(block, qkv, dout, table, dqkv, acc_k, acc_v):
    seq = qkv.shape[0]
    for start in reversed(range(0, seq, block)):
        attention_rows(start, block, qkv, dout, table, dqkv, acc_k, acc_v, start + block == seq)


ROWS = 128
UNIT = 16
UNITS = ROWS // UNIT
FIRST = 5
STEPS = 12


def units(count, step, start=0):
    def one(i, carry):
        step(i)
        return carry

    lax.fori_loop(start, start + count, one, 0)


def normalise(rows, tokens):
    wide = tokens[rows, :].astype(jnp.float32)
    inverse = lax.rsqrt(jnp.mean(wide * wide, axis=1, keepdims=True) + EPSILON)
    return wide * inverse, inverse


def step_kernel(
    reps,
    tokens_h, gain_h, wq_h, wk_h, wv_h, dout_h, table_h, global_h, local_h,
    gq_h, gk_h, gv_h, ggain_h, gtok_h, mean_h,
    tokens, gain, xf, weights, qkv, dqkv, dout, table, acc_k, acc_v,
    part, full_p, full_m, half_p, half_m, from_x,
    gq, gk, gv, gtok, gbuf, gsum, gfin,
    frag, buf_a, acc_a, buf_c, acc_c, buf_b, mean_a, mean_o, gpiece,
    load, store,
    asp, asm, asx, arp, arm, arx,
    rsp, rsm, rsx, rrp, rrm, rrx,
    gs, gr, fs, fr, fcs, fcr, fds, fdr,
):
    f32, bf = jnp.float32, jnp.bfloat16
    depth = xf.shape[1]
    mid = depth // 2
    r, t = lax.axis_index("rep"), lax.axis_index("tp")
    nz = reps // 4
    xh, z, core = r // (2 * nz), (r // 2) % nz, r % 2
    cx, y = t // 4, t % 4
    ox = 1 - cx
    up, dn, far = (y + 1) % 4, (y + 3) % 4, (y + 2) % 4

    def tp_dev(col, row):
        return (r, col * 4 + row)

    def rep_dev(h, zz, c):
        return (h * (2 * nz) + zz * 2 + c, t)

    dev_p, dev_m, dev_x = tp_dev(cx, up), tp_dev(cx, dn), tp_dev(ox, y)
    dev_core, dev_h = rep_dev(xh, z, 1 - core), rep_dev(1 - xh, z, core)

    def rdma(src, dst, s, d, dev):
        return pltpu.make_async_remote_copy(
            src_ref=src, dst_ref=dst, send_sem=s, recv_sem=d,
            device_id=dev, device_id_type=pl.DeviceIdType.MESH,
        )

    wide_q = wq_h.shape[1]
    loads = [
        (tokens_h, tokens),
        (gain_h, gain),
        (local_h, frag),
        (wq_h, weights.at[:, :wide_q]),
        (wk_h, weights.at[:, wide_q : wide_q + HEAD]),
        (wv_h, weights.at[:, wide_q + HEAD :]),
        (table_h, table),
        (dout_h, dout),
        (
            global_h.at[
                pl.ds(pl.multiple_of(core * 32 + xh * 16, 16), 16),
                pl.ds(pl.multiple_of(z * (depth // nz), 128), depth // nz),
            ],
            gpiece,
        ),
    ]
    loads = [pltpu.make_async_copy(a, b, load.at[i]) for i, (a, b) in enumerate(loads)]
    for c in loads:
        c.start()

    barrier = pltpu.get_barrier_semaphore()
    peers = [(r, (t + d) % 8) for d in range(1, 8)]
    peers += [dev_core, dev_h] + [rep_dev(xh, (z + d) % nz, core) for d in range(1, nz)]
    for p in peers:
        pl.semaphore_signal(barrier, inc=1, device_id=p, device_id_type=pl.DeviceIdType.MESH)
    loads[0].wait()
    loads[1].wait()
    loads[2].wait()
    pl.semaphore_wait(barrier, len(peers))

    def frag_a():
        other = pl.ds(pl.multiple_of((1 - core) * 32, 32), 32)
        return rdma(frag.at[other, :], buf_a, fs.at[0], fr.at[0], dev_core)

    frag_a().start()

    def place(ref, col, row, u, half=None):
        rows = pl.ds(pl.multiple_of((col * 4 + row) * ROWS + u * UNIT, UNIT), UNIT)
        if half is None:
            return ref.at[rows, :]
        return ref.at[rows, half * mid : (half + 1) * mid]

    def gather(way, i, col, row, u, half=None):
        s, d, dev = ((asp, arp, dev_p), (asm, arm, dev_m), (asx, arx, dev_x))[way]
        ref = place(xf, col, row, u, half)
        return rdma(ref, ref, s.at[i], d.at[i], dev)

    def norm_unit(i):
        u = (i + FIRST) % UNITS
        rows = pl.ds(pl.multiple_of(u * UNIT, UNIT), UNIT)
        xhat, _ = normalise(rows, tokens)
        at = pl.ds(pl.multiple_of(t * ROWS + u * UNIT, UNIT), UNIT)
        xf[at, :] = (xhat * gain[...]).astype(bf)

    def send_own(i):
        u = (i + FIRST) % UNITS
        for way in range(3):
            gather(way, u, cx, y, u).start()

    norm_unit(0)

    def norm_and_send(i):
        norm_unit(i)
        send_own(i - 1)

    units(UNITS - 1, norm_and_send, 1)
    for c in loads[3:]:
        c.wait()
    send_own(UNITS - 1)

    later = UNITS - FIRST

    def relay_later(i):
        u = FIRST + i
        gather(0, u, cx, dn, u).wait_recv()
        gather(0, 13 + u, cx, dn, u, 0).start()
        gather(2, 8 + i, cx, dn, u).start()
        gather(1, u, cx, up, u).wait_recv()
        gather(1, 13 + u, cx, up, u, 1).start()
        gather(2, 11 + i, cx, up, u).start()

    def relay_first(u):
        gather(0, u, cx, dn, u).wait_recv()
        gather(0, 13 + u, cx, dn, u, 0).start()
        gather(1, u, cx, up, u).wait_recv()
        gather(1, 13 + u, cx, up, u, 1).start()
        gather(2, u, ox, y, u).wait_recv()
        gather(0, 8 + u, ox, y, u).start()
        gather(1, 8 + u, ox, y, u).start()

    def relay_far(i):
        u = FIRST + i
        gather(0, 13 + u, cx, far, u, 0).wait_recv()
        gather(1, 13 + u, cx, far, u, 1).wait_recv()
        gather(2, 14 + i, cx, far, u).start()

    def relay_other(u):
        gather(0, 8 + u, ox, dn, u).wait_recv()
        gather(0, 21 + u, ox, dn, u, 0).start()
        gather(1, 8 + u, ox, up, u).wait_recv()
        gather(1, 21 + u, ox, up, u, 1).start()

    zcols = depth // nz

    def frag_c(d):
        peer = (z + d) % nz
        return rdma(
            acc_a.at[:, pl.ds(pl.multiple_of(peer * zcols, 128), zcols)], buf_c.at[z],
            fcs.at[d], fcr.at[d], rep_dev(xh, peer, core),
        )

    def frag_b():
        other = pl.ds(pl.multiple_of((1 - xh) * 16, 16), 16)
        return rdma(acc_c.at[other, :], buf_b, fs.at[1], fr.at[1], dev_h)

    def frag_b_back():
        mine = mean_a.at[z, pl.ds(pl.multiple_of(xh * 16, 16), 16), :]
        return rdma(mine, mine, fs.at[2], fr.at[2], dev_h)

    def frag_c_back(d):
        return rdma(mean_a.at[z], mean_a.at[z], fds.at[d], fdr.at[d], rep_dev(xh, (z + d) % nz, core))

    def frag_a_back():
        return rdma(mean_a, mean_o, fs.at[3], fr.at[3], dev_core)

    def frag_step(k):
        if k == 0:
            frag_a().wait_recv()
            own = frag[pl.ds(pl.multiple_of(core * 32, 32), 32), :]
            acc_a[...] = own.astype(f32) + buf_a[...].astype(f32)
        elif k == 1:
            for d in range(1, nz):
                frag_c(d).start()
        elif k == 2:
            for d in range(1, nz):
                frag_c(d).wait_recv()
            total = acc_a[:, pl.ds(pl.multiple_of(z * zcols, 128), zcols)]
            for d in range(1, nz):
                total += buf_c[(z + d) % nz]
            acc_c[...] = total
        elif k == 3:
            frag_b().start()
        elif k == 4:
            frag_b().wait_recv()
            rows = pl.ds(pl.multiple_of(xh * 16, 16), 16)
            mean_a[z, rows, :] = gpiece[...] - (acc_c[rows, :] + buf_b[...]) * (1.0 / reps)
        elif k == 5:
            frag_b_back().start()
        elif k == 6:
            other = mean_a.at[z, pl.ds(pl.multiple_of((1 - xh) * 16, 16), 16), :]
            rdma(other, other, fs.at[2], fr.at[2], dev_h).wait_recv()
            for d in range(1, nz):
                frag_c_back(d).start()
        elif k == 7:
            for d in range(1, nz):
                slot = mean_a.at[(z + nz - d) % nz]
                rdma(slot, slot, fds.at[d], fdr.at[d], rep_dev(xh, (z + d) % nz, core)).wait_recv()
            frag_a_back().start()
        elif k == 8:
            frag_a_back().wait_recv()

    def mean_out(zz, c):
        which, src = ((core, mean_a), (1 - core, mean_o))[c]
        return pltpu.make_async_copy(
            src.at[zz],
            mean_h.at[pl.ds(pl.multiple_of(which * 32, 32), 32), zz * zcols : (zz + 1) * zcols],
            store.at[6 + 2 * zz + c],
        )

    def gather_stage(s):
        @pl.when(s == 0)
        def _():
            frag_step(0)

        @pl.when(s == 1)
        def _():
            frag_step(1)
            units(later, relay_later)
            units(FIRST, relay_first)
            units(later, lambda i: gather(2, FIRST + i, ox, y, FIRST + i).wait_recv())

        @pl.when(s == 2)
        def _():
            frag_step(2)

        @pl.when(s == 3)
        def _():
            frag_step(3)

        @pl.when(s == 4)
        def _():
            units(later, relay_far)
            frag_step(4)
            units(FIRST, relay_other)
            frag_step(5)

            def landed(u):
                gather(0, 13 + u, cx, far, u, 0).wait_recv()
                gather(1, 13 + u, cx, far, u, 1).wait_recv()

            units(FIRST, landed)

        @pl.when(s == 5)
        def _():
            frag_step(6)
            units(later, lambda i: gather(2, 8 + i, ox, dn, FIRST + i).wait_recv())

        @pl.when(s == 6)
        def _():
            units(later, lambda i: gather(2, 11 + i, ox, up, FIRST + i).wait_recv())

        @pl.when(s == 7)
        def _():
            def landed(u):
                gather(0, 21 + u, ox, far, u, 0).wait_recv()
                gather(1, 21 + u, ox, far, u, 1).wait_recv()

            units(FIRST, landed)
            units(later, lambda i: gather(2, 14 + i, ox, far, FIRST + i).wait_recv())

        k = (s + 1) % 3
        d = 3 - 2 * k + 3 * (k * (k - 1) // 2)
        beyond = (s + 6) // 8
        row = (y + d * beyond) % 4
        other = (1 - beyond) * (s % 2) + beyond * ((s + 3) // 8)
        col = cx + other * (1 - 2 * cx)
        at = pl.ds(pl.multiple_of((col * 4 + row) * ROWS, ROWS), ROWS)
        project(at, xf[at, :], weights, table, qkv)

    units(8, gather_stage)

    attention(256, qkv, dout, table, dqkv, acc_k, acc_v)

    def scatter(way, i, src, dst):
        s, d, dev = ((rsp, rrp, dev_p), (rsm, rrm, dev_m), (rsx, rrx, dev_x))[way]
        return rdma(src, dst, s.at[i], d.at[i], dev)

    def slot(ref, i):
        return ref.at[pl.ds(pl.multiple_of(i * UNIT, UNIT), UNIT), :]

    def scatter_full(way, i, col, row, u):
        return scatter(way, i, place(part, col, row, u), slot((full_p, full_m)[way], i))

    def scatter_half(way, i, col, row, u):
        half = 1 - way
        return scatter(way, 13 + i, place(part, col, row, u, half), slot((half_p, half_m)[way], i))

    def scatter_x(i, col, row, u):
        return scatter(2, i, place(part, col, row, u), slot(from_x, i))

    def add(col, row, u, terms, half=None):
        rows = pl.ds(pl.multiple_of((col * 4 + row) * ROWS + u * UNIT, UNIT), UNIT)
        cols = slice(0, depth) if half is None else slice(half * mid, (half + 1) * mid)
        total = part[rows, cols].astype(f32)
        for ref, i in terms:
            total += ref[pl.ds(pl.multiple_of(i * UNIT, UNIT), UNIT), :].astype(f32)
        part[rows, cols] = total.astype(bf)

    def near(i, col, u):
        scatter_half(0, i, col, far, u).wait_recv()
        add(col, up, u, [(half_p, i)], 1)
        scatter_half(1, i, col, far, u).wait_recv()
        add(col, dn, u, [(half_m, i)], 0)
        scatter_full(0, i, col, up, u).start()
        scatter_full(1, i, col, dn, u).start()

    def across(i):
        scatter_full(0, i, ox, y, i).wait_recv()
        scatter_full(1, i, ox, y, i).wait_recv()
        add(ox, y, i, [(full_p, i), (full_m, i)])
        scatter_x(12 + i, ox, y, i).start()

    def far_halves(i, col, u):
        scatter_half(0, i, col, far, u).start()
        scatter_half(1, i, col, far, u).start()

    def far_later(i):
        u = FIRST + i
        scatter_x(i, cx, far, u).wait_recv()
        add(cx, far, u, [(from_x, i)])
        far_halves(5 + u, cx, u)

    def side_later(i):
        u = FIRST + i
        scatter_x(3 + i, cx, up, u).wait_recv()
        add(cx, up, u, [(from_x, 3 + i)])
        scatter_x(6 + i, cx, dn, u).wait_recv()
        add(cx, dn, u, [(from_x, 6 + i)])

    def part_stage(s):
        k = s % 4
        d = 2 - k + 3 * (k // 2) - 2 * (k // 3)
        row = (y + d) % 4
        col = ox + (s // 4) * (1 - 2 * ox)
        at = pl.ds(pl.multiple_of((col * 4 + row) * ROWS, ROWS), ROWS)
        part[at, :] = dot_t(dqkv[at, :], weights[...]).astype(bf)

        @pl.when(s < 4)
        def _():
            units(later, lambda i: scatter_x(3 * s + i, ox, row, FIRST + i).start())

        @pl.when(s == 0)
        def _():
            units(FIRST, lambda u: far_halves(u, ox, u))

        @pl.when(s == 4)
        def _():
            units(FIRST, lambda u: far_halves(5 + u, cx, u))

        @pl.when(s == 5)
        def _():
            units(FIRST, lambda u: near(u, ox, u))

        @pl.when(s == 6)
        def _():
            frag_step(7)

    units(8, part_stage)

    def weight_stage(j):
        @pl.when(j == 1)
        def _():
            units(later, far_later)

        @pl.when(j == 3)
        def _():
            units(FIRST, lambda u: near(5 + u, cx, u))

        @pl.when(j == 5)
        def _():
            units(FIRST, across)

        @pl.when(j == 7)
        def _():
            units(later, side_later)

        @pl.when(j == 8)
        def _():
            units(later, lambda i: near(5 + FIRST + i, cx, FIRST + i))

        @pl.when(j == 9)
        def _():
            frag_step(8)
            for zz in range(nz):
                for c in range(2):
                    mean_out(zz, c).start()

        block = depth // STEPS
        at = pl.ds(pl.multiple_of(j * block, block), block)
        g = t_dot(xf[:, at], dqkv[...]).astype(bf)
        gq[at, :] = g[:, :wide_q]
        gk[at, :] = g[:, wide_q : wide_q + HEAD]
        gv[at, :] = g[:, wide_q + HEAD :]

    units(STEPS, weight_stage)
    stores = [(gq, gq_h), (gk, gk_h), (gv, gv_h)]
    stores = [pltpu.make_async_copy(a, b, store.at[i]) for i, (a, b) in enumerate(stores)]
    for c in stores:
        c.start()

    gsum[...] = jnp.zeros_like(gsum)

    def finish(u):
        @pl.when(u < FIRST)
        def _():
            scatter_x(12 + u, cx, y, u).wait_recv()

        @pl.when(u >= FIRST)
        def _():
            scatter_x(9 + u - FIRST, cx, y, u).wait_recv()

        at_x = (12 + u) * (1 - u // FIRST) + (4 + u) * (u // FIRST)
        scatter_full(0, 5 + u, cx, y, u).wait_recv()
        scatter_full(1, 5 + u, cx, y, u).wait_recv()

        def term(ref, i):
            return ref[pl.ds(pl.multiple_of(i * UNIT, UNIT), UNIT), :].astype(f32)

        mine = (cx * 4 + y) * UNITS + u
        total = (term(part, mine) + term(from_x, at_x)) + (term(full_p, 5 + u) + term(full_m, 5 + u))
        rows = pl.ds(pl.multiple_of(u * UNIT, UNIT), UNIT)
        xhat, inverse = normalise(rows, tokens)
        gsum[...] += total * xhat
        scaled = total * gain[...]
        mean = jnp.mean(scaled * xhat, axis=1, keepdims=True)
        gtok[rows, :] = (inverse * (scaled - xhat * mean)).astype(bf)

    units(UNITS, finish)
    gbuf[t] = jnp.sum(gsum[...], axis=0, keepdims=True)
    out_tokens = pltpu.make_async_copy(gtok, gtok_h, store.at[3])
    out_tokens.start()

    def gain_to(d):
        return rdma(gbuf.at[t], gbuf.at[t], gs.at[d], gr.at[d], (r, (t + d) % 8))

    for d in range(1, 8):
        gain_to(d).start()
    for d in range(1, 8):
        ref = gbuf.at[(t + 8 - d) % 8]
        rdma(ref, ref, gs.at[d], gr.at[d], (r, (t + d) % 8)).wait_recv()
    total = gbuf[0]
    for d in range(1, 8):
        total += gbuf[d]
    gfin[...] = total
    out_gain = pltpu.make_async_copy(gfin, ggain_h, store.at[4])
    out_gain.start()

    units(8, lambda i: [gather(w, i, cx, y, i).wait_send() for w in range(3)] and None)
    units(FIRST, lambda i: [gather(w, 8 + i, ox, y, i).wait_send() for w in range(2)] and None)
    units(13, lambda i: [gather(w, 13 + i, cx, y, 0, w).wait_send() for w in range(2)] and None)
    units(9, lambda i: gather(2, 8 + i, cx, y, 0).wait_send())
    units(13, lambda i: [scatter_full(w, i, cx, y, 0).wait_send() for w in range(2)] and None)
    units(13, lambda i: [scatter_half(w, i, cx, y, 0).wait_send() for w in range(2)] and None)
    units(17, lambda i: scatter_x(i, cx, y, 0).wait_send())
    for d in range(1, 8):
        gain_to(d).wait_send()
    for d in range(1, nz):
        frag_c(d).wait_send()
        frag_c_back(d).wait_send()
    frag_a().wait_send()
    frag_b().wait_send()
    frag_b_back().wait_send()
    frag_a_back().wait_send()
    for c in stores + [out_tokens, out_gain]:
        c.wait()
    for zz in range(nz):
        for c in range(2):
            mean_out(zz, c).wait()


def run(reps, tokens, gain, wq, wk, wv, dout, global_fragment, local_fragment):
    depth = tokens.shape[1]
    seq = dout.shape[0]
    table = rope_constants(seq)
    f32, bf = jnp.float32, jnp.bfloat16
    cols = wq.shape[1] + wk.shape[1] + wv.shape[1]
    anywhere = pl.BlockSpec(memory_space=pl.ANY)
    nz = reps // 4
    zcols = depth // nz
    dma = pltpu.SemaphoreType.DMA
    vm = pltpu.VMEM
    scratch = [
        vm((ROWS, depth), bf), vm((1, depth), f32), vm((seq, depth), bf), vm((depth, cols), bf),
        vm((seq, cols), bf), vm((seq, cols), bf), vm(dout.shape, bf), vm(table.shape, f32),
        vm((seq, HEAD), f32), vm((seq, HEAD), f32),
        vm((seq, depth), bf),
        vm((13 * UNIT, depth), bf), vm((13 * UNIT, depth), bf),
        vm((13 * UNIT, depth // 2), bf), vm((13 * UNIT, depth // 2), bf), vm((17 * UNIT, depth), bf),
        vm(wq.shape, bf), vm(wk.shape, bf), vm(wv.shape, bf), vm((ROWS, depth), bf),
        vm((8, 1, depth), f32), vm((UNIT, depth), f32), vm((1, depth), f32),
        vm((64, depth), bf), vm((32, depth), bf), vm((32, depth), f32), vm((nz, 32, zcols), f32),
        vm((32, zcols), f32), vm((16, zcols), f32), vm((nz, 32, zcols), f32), vm((nz, 32, zcols), f32),
        vm((16, zcols), f32),
        dma((9,)), dma((6 + 2 * nz,)),
    ]
    scratch += [dma((n,)) for n in (26, 26, 17) * 4]
    scratch += [dma((n,)) for n in (8, 8, 4, 4, nz, nz, nz, nz)]
    return pl.pallas_call(
        functools.partial(step_kernel, reps),
        out_shape=(
            jax.ShapeDtypeStruct(wq.shape, bf),
            jax.ShapeDtypeStruct(wk.shape, bf),
            jax.ShapeDtypeStruct(wv.shape, bf),
            jax.ShapeDtypeStruct((1, depth), f32),
            jax.ShapeDtypeStruct((ROWS, depth), bf),
            jax.ShapeDtypeStruct((64, depth), f32),
        ),
        in_specs=[anywhere] * 9,
        out_specs=[anywhere] * 6,
        scratch_shapes=scratch,
        compiler_params=pltpu.CompilerParams(
            vmem_limit_bytes=60 * 1024 * 1024, collective_id=0, has_side_effects=True
        ),
    )(tokens, gain, wq, wk, wv, dout, table, global_fragment, local_fragment)


def body(tokens, norm_gain, w_query, key_weight, value_weight, attention_gradient, global_fragment, momentum, local_fragment):
    replicas = lax.axis_size("rep")
    gq, gk, gv, grad_gain, grad_tokens, mean = run(
        replicas, tokens[0], norm_gain, w_query[0], key_weight[0], value_weight[0],
        attention_gradient[0], global_fragment, local_fragment[0],
    )
    new_momentum = OUTER_MOMENTUM * momentum + mean
    new_global = global_fragment - OUTER_RATE * (mean + OUTER_MOMENTUM * new_momentum)
    return (gq[None], gk[None], gv[None], grad_gain, grad_tokens[None], new_global, new_momentum)


def solution(mesh):
    placed = (
        P("rep", "tp", None), P("rep", None), P("rep", None, "tp"), P("rep", None, "tp"), P("rep", None, "tp"),
        P("rep", None, "tp"), P("tp", None), P("tp", None), P("rep", "tp", None),
    )
    outs = (P("rep", None, "tp"), P("rep", None, "tp"), P("rep", None, "tp"), P("rep", None), P("rep", "tp", None), P("tp", None), P("tp", None))
    return jax.shard_map(body, mesh=mesh, in_specs=placed, out_specs=outs, check_vma=False)
```

time: 239 us -> 121 us (0.51); the launches traced: 236 us -> 120 us
  waiting for transfers between devices: 102 us -> 0 us
  Pallas kernels: 28.6 us -> 112 us
  blocking collectives: 69.4 us -> 0 us
  between operations: 14.1 us -> 0.69 us
  starting transfers between devices: 9.89 us -> 0 us
  other arithmetic: 9.07 us -> 2.59 us
  local copies, waits for them, and re-layouts: 2.45 us -> 4.94 us
    pallas_call x1, Pallas kernels: 28.6 us -> 112 us  [run(): pl.pallas_call(functools.partial(step_kernel, reps), out_shape=(jax.Shape...]
    all_gather x1 -> x0, waiting for transfers between devices: 75.5 us -> none  [body(): lax.all_gather((xhat * gain[None, :]).astype(jnp.bfloat16), 'tp', axis=0,...]
    all_gather x2 -> x0, blocking collectives: 69.4 us -> none  [the longest x1 39.4 us: body(): mean = lax.all_gather(mean_rows, 'rep', axis=0, tiled=True)]
    all_to_all x1 -> x0, waiting for transfers between devices: 17.3 us -> none  [body(): lax.all_to_all(mine, 'rep', split_axis=0, concat_axis=0, tiled=True)]
    all_to_all x1 -> x0, starting transfers between devices: 9.81 us -> none  [body(): lax.all_to_all(mine, 'rep', split_axis=0, concat_axis=0, tiled=True)]
    reduce_scatter x1 -> x0, waiting for transfers between devices: 9.21 us -> none  [body(): lax.psum_scatter(part, 'tp', scatter_dimension=0, tiled=True)]
    reduce_sum x4 -> x0, other arithmetic: 4.1 us -> none  [the longest x1 1.78 us: body(): jnp.mean(scaled * xhat, axis=-1, keepdims=True)]
    unnamed x13 -> x19, local copies, waits for them, and re-layouts: 1.54 us -> 4.94 us
  transfers between devices with their start and end apart: 3 -> 0, of which waited for: 3 -> 0; matrix products, arithmetic and copies ran while one was open for 1% -> 0% of each run, Pallas kernels for 0% -> 0%
where the time goes in v2:
time: 121 us; the launch traced here: 120 us
  Pallas kernels  112 us (93%)
  local copies, waits for them, and re-layouts  4.94 us (4%)
  other arithmetic  2.59 us (2%)
    pallas_call x1, Pallas kernels, run(): pl.pallas_call(functools.partial(step_kernel, reps), out_shape=(jax.Shape...  112 us
    unnamed x19, local copies, waits for them, and re-layouts  4.94 us
    sub x1, other arithmetic, body(): global_fragment - OUTER_RATE * (mean + OUTER_MOMENTUM * new_momentum)  2.59 us

profile of v2, /device:TPU:8, one launch (start us, length us, event | category | flops | bytes accessed | tf_op | source)
XLA Modules:
  0.0 120.0 jit_solution(5103843435035024988)
XLA Ops:
  0.6 0.0 copy-start
  0.6 0.0 copy-start.5
  0.7 111.8 %shard_map.153 = (bf16[3072,256]{1,0:T(8,128)(2,1)}, bf16[3072,128]{1,0:T(8,128)(2,1)}, bf16[3072,128]{1,0:T(8,128)(2,1)}, f32[1,3072]{1,0:T(1,128)}, bf16[128,3072]{1,0:T(8,128)(2,1)}, /*index=5*/f32[64,3072]{1,0:T(8,128)}) custom-call(bf16[128,3072]{1,0:T(8,128)(2,1)} %bitcast.15, f32[1,3072]{1,0:T(1,128)} %gain_h.1, bf16[3072,256]{1,0:T(8,128)(2,1)} %bitcast.11, ...), custom_call_target="tpu_custom_call" | custom-call | tf_op jit(solution)/shard_map/pallas_call | solution.py:623
  112.5 0.0 copy-done
  112.5 0.0 copy-done.5
  112.5 0.0 copy-start.1
  112.5 2.6 %multiply_subtract_fusion = (f32[64,3072]{1,0:T(8,128)}, f32[64,3072]{1,0:T(8,128)}) fusion(f32[64,3072]{1,0:T(8,128)S(1)} %copy-done, f32[64,3072]{1,0:T(8,128)} %get-tuple-element.18, f32[64,3072]{1,0:T(8,128)S(1)} %copy-done.5), kind=kLoop, calls=%fused_computation | loop fusion | flops 1179648 | bytes 3932160 | tf_op jit(solution)/shard_map/sub | solution.py:649
  115.1 0.0 copy-done.1
  115.1 0.0 copy-start.4
  115.1 0.0 copy-start.3
  115.1 1.1 copy.22
  116.2 0.5 copy-done.4
  116.8 0.0 copy-start.6
  116.8 0.0 copy-start.2
  116.8 0.9 copy.23
  117.7 0.0 copy-done.3
  117.7 0.9 copy.24
  118.5 0.0 copy-done.6
  118.5 0.6 copy.25
  119.1 0.0 copy-done.2
  119.1 0.9 copy.26
Async XLA Ops:
  0.6 111.8 %copy-start = (f32[64,3072]{1,0:T(8,128)S(1)}, f32[64,3072]{1,0:T(8,128)}, u32[]{:S(2)}) copy-start(f32[64,3072]{1,0:T(8,128)} %global_h.1) | copy-start | bytes 2359300
  0.6 111.8 %copy-start.5 = (f32[64,3072]{1,0:T(8,128)S(1)}, f32[64,3072]{1,0:T(8,128)}, u32[]{:S(2)}) copy-start(f32[64,3072]{1,0:T(8,128)} %param.17) | copy-start | bytes 2359300
  112.5 2.6 %copy-start.1 = (bf16[3072,256]{1,0:T(8,128)(2,1)S(1)}, bf16[3072,256]{1,0:T(8,128)(2,1)}, u32[]{:S(2)}) copy-start(bf16[3072,256]{1,0:T(8,128)(2,1)} %get-tuple-element.13) | copy-start | bytes 4718596
  115.1 1.7 %copy-start.4 = (bf16[3072,128]{1,0:T(8,128)(2,1)S(1)}, bf16[3072,128]{1,0:T(8,128)(2,1)}, u32[]{:S(2)}) copy-start(bf16[3072,128]{1,0:T(8,128)(2,1)} %get-tuple-element.14) | copy-start | bytes 2359300
  115.1 2.6 %copy-start.3 = (bf16[3072,128]{1,0:T(8,128)(2,1)S(1)}, bf16[3072,128]{1,0:T(8,128)(2,1)}, u32[]{:S(2)}) copy-start(bf16[3072,128]{1,0:T(8,128)(2,1)} %get-tuple-element.15) | copy-start | bytes 2359300
  116.8 1.8 %copy-start.6 = (f32[1,3072]{1,0:T(1,128)S(1)}, f32[1,3072]{1,0:T(1,128)}, u32[]{:S(2)}) copy-start(f32[1,3072]{1,0:T(1,128)} %get-tuple-element.31) | copy-start | bytes 36868
  116.8 2.4 %copy-start.2 = (bf16[128,3072]{1,0:T(8,128)(2,1)S(1)}, bf16[128,3072]{1,0:T(8,128)(2,1)}, u32[]{:S(2)}) copy-start(bf16[128,3072]{1,0:T(8,128)(2,1)} %get-tuple-element.17) | copy-start | bytes 2359300

commit v3 on v2

--- a/solution.py
+++ b/solution.py
@@ -56,32 +56,34 @@
 def attention_rows(start, block, qkv, dout, table, dqkv, acc_k, acc_v, first):
     width = start + block
     scale = HEAD ** (-0.5)
+    power_scale = scale * 1.4426950408889634
     heads = dout.shape[1] // HEAD
     at_k, at_v = heads * HEAD, (heads + 1) * HEAD
     keys = qkv[:width, at_k : at_k + HEAD]
     values = qkv[:width, at_v : at_v + HEAD]
     rows = slice(start, start + block)
-    row = lax.broadcasted_iota(jnp.int32, (block, block), 0)
-    col = lax.broadcasted_iota(jnp.int32, (block, block), 1)
-    allowed = col <= row
+    key = lax.broadcasted_iota(jnp.int32, (block, block), 0)
+    query = lax.broadcasted_iota(jnp.int32, (block, block), 1)
+    allowed = key <= query
     cos, sin = table[rows, :HEAD], table[rows, HEAD:]
     dk = dv = None
     for h in range(heads):
         q = qkv[rows, h * HEAD : (h + 1) * HEAD]
         do = dout[rows, h * HEAD : (h + 1) * HEAD]
-        s = dot_t(q, keys)
-        last = jnp.where(allowed, s[:, start:], NEGATIVE)
-        s = last if start == 0 else jnp.concatenate([s[:, :start], last], axis=1)
-        top = jnp.max(s, axis=1, keepdims=True)
-        power = jnp.exp((s - top) * scale)
-        p = power * (1.0 / jnp.sum(power, axis=1, keepdims=True))
-        dp = dot_t(do, values)
-        drop = jnp.sum(dp * p, axis=1, keepdims=True)
-        ds = ((p * (dp - drop)) * scale).astype(jnp.bfloat16)
-        p_low = p.astype(jnp.bfloat16)
-        dq = jnp.dot(ds, keys, preferred_element_type=jnp.float32)
+        s = dot_t(keys, q)
+        last = jnp.where(allowed, s[start:, :], NEGATIVE)
+        s = last if start == 0 else jnp.concatenate([s[:start, :], last], axis=0)
+        top = jnp.max(s, axis=0, keepdims=True)
+        power = jnp.exp2((s - top) * power_scale)
+        inverse = 1.0 / jnp.sum(power, axis=0, keepdims=True)
+        p_low = (power * inverse).astype(jnp.bfloat16)
+        dp = dot_t(values, do)
+        drop = jnp.sum(dp * power, axis=0, keepdims=True) * inverse
+        ds = (power * ((dp - drop) * (inverse * scale))).astype(jnp.bfloat16)
+        dq = t_dot(keys, ds).T
         dqkv[rows, h * HEAD : (h + 1) * HEAD] = unrope(dq, cos, sin).astype(jnp.bfloat16)
-        tv, tk = t_dot(p_low, do), t_dot(ds, q)
+        tv = jnp.dot(p_low, do, preferred_element_type=jnp.float32)
+        tk = jnp.dot(ds, q, preferred_element_type=jnp.float32)
         dv = tv if dv is None else dv + tv
         dk = tk if dk is None else dk + tk
     if first:
@@ -90,23 +92,17 @@
     else:
         acc_v[:width, :] += dv
         acc_k[:width, :] += dk
-    width = start
-    heads_at = heads * HEAD
-    dqkv[rows, heads_at : heads_at + HEAD] = unrope(acc_k[rows, :], cos, sin).astype(jnp.bfloat16)
-    dqkv[rows, heads_at + HEAD : heads_at + 2 * HEAD] = acc_v[rows, :].astype(jnp.bfloat16)
-
-
-def attention(block, qkv, dout, table, dqkv, acc_k, acc_v):
-    seq = qkv.shape[0]
-    for start in reversed(range(0, seq, block)):
-        attention_rows(start, block, qkv, dout, table, dqkv, acc_k, acc_v, start + block == seq)
+    dqkv[rows, at_k : at_k + HEAD] = unrope(acc_k[rows, :], cos, sin).astype(jnp.bfloat16)
+    dqkv[rows, at_v : at_v + HEAD] = acc_v[rows, :].astype(jnp.bfloat16)
 
 
 ROWS = 128
 UNIT = 16
 UNITS = ROWS // UNIT
+BLOCK = 256
 FIRST = 5
 STEPS = 12
+LIMIT = 44 * 1024 * 1024
 
 
 def units(count, step, start=0):
@@ -125,13 +121,13 @@
 
 def step_kernel(
     reps,
-    tokens_h, gain_h, wq_h, wk_h, wv_h, dout_h, table_h, global_h, local_h,
-    gq_h, gk_h, gv_h, ggain_h, gtok_h, mean_h,
+    tokens_h, gain_h, wq_h, wk_h, wv_h, dout_h, table_h, global_h, momentum_h, local_h,
+    gq, gk, gv, ggain, gtok, new_global, new_momentum,
     tokens, gain, xf, weights, qkv, dqkv, dout, table, acc_k, acc_v,
     part, full_p, full_m, half_p, half_m, from_x,
-    gq, gk, gv, gtok, gbuf, gsum, gfin,
-    frag, buf_a, acc_a, buf_c, acc_c, buf_b, mean_a, mean_o, gpiece,
-    load, store,
+    gbuf, gsum,
+    frag, buf_a, acc_a, buf_c, acc_c, buf_b, mean_a, mean_o, glob, mom,
+    load,
     asp, asm, asx, arp, arm, arx,
     rsp, rsm, rsx, rrp, rrm, rrx,
     gs, gr, fs, fr, fcs, fcr, fds, fdr,
@@ -171,13 +167,8 @@
         (wv_h, weights.at[:, wide_q + HEAD :]),
         (table_h, table),
         (dout_h, dout),
-        (
-            global_h.at[
-                pl.ds(pl.multiple_of(core * 32 + xh * 16, 16), 16),
-                pl.ds(pl.multiple_of(z * (depth // nz), 128), depth // nz),
-            ],
-            gpiece,
-        ),
+        (global_h, glob),
+        (momentum_h, mom),
     ]
     loads = [pltpu.make_async_copy(a, b, load.at[i]) for i, (a, b) in enumerate(loads)]
     for c in loads:
@@ -190,14 +181,20 @@
         pl.semaphore_signal(barrier, inc=1, device_id=p, device_id_type=pl.DeviceIdType.MESH)
     loads[0].wait()
     loads[1].wait()
+
+    def norm_unit(u):
+        rows = pl.ds(pl.multiple_of(u * UNIT, UNIT), UNIT)
+        xhat, _ = normalise(rows, tokens)
+        at = pl.ds(pl.multiple_of(t * ROWS + u * UNIT, UNIT), UNIT)
+        xf[at, :] = (xhat * gain[...]).astype(bf)
+
+    units(UNITS, norm_unit)
     loads[2].wait()
     pl.semaphore_wait(barrier, len(peers))
 
     def frag_a():
         other = pl.ds(pl.multiple_of((1 - core) * 32, 32), 32)
         return rdma(frag.at[other, :], buf_a, fs.at[0], fr.at[0], dev_core)
-
-    frag_a().start()
 
     def place(ref, col, row, u, half=None):
         rows = pl.ds(pl.multiple_of((col * 4 + row) * ROWS + u * UNIT, UNIT), UNIT)
@@ -210,28 +207,16 @@
         ref = place(xf, col, row, u, half)
         return rdma(ref, ref, s.at[i], d.at[i], dev)
 
-    def norm_unit(i):
-        u = (i + FIRST) % UNITS
-        rows = pl.ds(pl.multiple_of(u * UNIT, UNIT), UNIT)
-        xhat, _ = normalise(rows, tokens)
-        at = pl.ds(pl.multiple_of(t * ROWS + u * UNIT, UNIT), UNIT)
-        xf[at, :] = (xhat * gain[...]).astype(bf)
-
     def send_own(i):
         u = (i + FIRST) % UNITS
         for way in range(3):
             gather(way, u, cx, y, u).start()
 
-    norm_unit(0)
-
-    def norm_and_send(i):
-        norm_unit(i)
-        send_own(i - 1)
-
-    units(UNITS - 1, norm_and_send, 1)
+    units(UNITS, send_own)
+    frag_a().start()
+    gsum[...] = jnp.zeros_like(gsum)
     for c in loads[3:]:
         c.wait()
-    send_own(UNITS - 1)
 
     later = UNITS - FIRST
 
@@ -308,7 +293,13 @@
         elif k == 4:
             frag_b().wait_recv()
             rows = pl.ds(pl.multiple_of(xh * 16, 16), 16)
-            mean_a[z, rows, :] = gpiece[...] - (acc_c[rows, :] + buf_b[...]) * (1.0 / reps)
+            mean_a[z, rows, :] = (
+                glob[
+                    pl.ds(pl.multiple_of(core * 32 + xh * 16, 16), 16),
+                    pl.ds(pl.multiple_of(z * zcols, 128), zcols),
+                ]
+                - (acc_c[rows, :] + buf_b[...]) * (1.0 / reps)
+            )
         elif k == 5:
             frag_b_back().start()
         elif k == 6:
@@ -324,13 +315,14 @@
         elif k == 8:
             frag_a_back().wait_recv()
 
-    def mean_out(zz, c):
-        which, src = ((core, mean_a), (1 - core, mean_o))[c]
-        return pltpu.make_async_copy(
-            src.at[zz],
-            mean_h.at[pl.ds(pl.multiple_of(which * 32, 32), 32), zz * zcols : (zz + 1) * zcols],
-            store.at[6 + 2 * zz + c],
-        )
+    def outer_update(zz):
+        cols = slice(zz * zcols, (zz + 1) * zcols)
+        for which, src in ((core, mean_a), (1 - core, mean_o)):
+            rows = pl.ds(pl.multiple_of(which * 32, 32), 32)
+            mean = src[zz]
+            moved = OUTER_MOMENTUM * mom[rows, cols] + mean
+            new_momentum[rows, cols] = moved
+            new_global[rows, cols] = glob[rows, cols] - OUTER_RATE * (mean + OUTER_MOMENTUM * moved)
 
     def gather_stage(s):
         @pl.when(s == 0)
@@ -394,8 +386,6 @@
 
     units(8, gather_stage)
 
-    attention(256, qkv, dout, table, dqkv, acc_k, acc_v)
-
     def scatter(way, i, src, dst):
         s, d, dev = ((rsp, rrp, dev_p), (rsm, rrm, dev_m), (rsx, rrx, dev_x))[way]
         return rdma(src, dst, s.at[i], d.at[i], dev)
@@ -441,46 +431,54 @@
 
     def far_later(i):
         u = FIRST + i
-        scatter_x(i, cx, far, u).wait_recv()
-        add(cx, far, u, [(from_x, i)])
+        scatter_x(3 + i, cx, far, u).wait_recv()
+        add(cx, far, u, [(from_x, 3 + i)])
         far_halves(5 + u, cx, u)
 
     def side_later(i):
         u = FIRST + i
-        scatter_x(3 + i, cx, up, u).wait_recv()
-        add(cx, up, u, [(from_x, 3 + i)])
+        scatter_x(i, cx, up, u).wait_recv()
+        add(cx, up, u, [(from_x, i)])
         scatter_x(6 + i, cx, dn, u).wait_recv()
         add(cx, dn, u, [(from_x, 6 + i)])
 
-    def part_stage(s):
-        k = s % 4
-        d = 2 - k + 3 * (k // 2) - 2 * (k // 3)
-        row = (y + d) % 4
-        col = ox + (s // 4) * (1 - 2 * ox)
-        at = pl.ds(pl.multiple_of((col * 4 + row) * ROWS, ROWS), ROWS)
-        part[at, :] = dot_t(dqkv[at, :], weights[...]).astype(bf)
-
-        @pl.when(s < 4)
-        def _():
-            units(later, lambda i: scatter_x(3 * s + i, ox, row, FIRST + i).start())
-
-        @pl.when(s == 0)
-        def _():
-            units(FIRST, lambda u: far_halves(u, ox, u))
-
-        @pl.when(s == 4)
-        def _():
-            units(FIRST, lambda u: far_halves(5 + u, cx, u))
-
-        @pl.when(s == 5)
-        def _():
-            units(FIRST, lambda u: near(u, ox, u))
-
-        @pl.when(s == 6)
-        def _():
-            frag_step(7)
-
-    units(8, part_stage)
+    def terms(chunk):
+        col, row = chunk // 4, chunk % 4
+        away = (row + 4 - y) % 4
+        other = (col + cx) % 2
+        at = pl.ds(pl.multiple_of(chunk * ROWS, ROWS), ROWS)
+        width = min(512, depth)
+        for j in range(0, depth, width):
+            cols = slice(j, j + width)
+            low = dot_t(dqkv[at, :], weights[cols, :]).astype(bf)
+            part[at, cols] = low
+            moved = low.astype(f32) * xf[at, cols].astype(f32)
+            gsum[:, cols] += jnp.sum(moved.reshape(ROWS // 8, 8, width), axis=0)
+
+        @pl.when(other == 1)
+        def _():
+            role = (away + 3) % 4
+            units(later, lambda i: scatter_x(3 * role + i, ox, row, FIRST + i).start())
+
+        @pl.when(away == 2)
+        def _():
+            units(FIRST, lambda u: far_halves(5 * (1 - other) + u, col, u))
+
+    seq = qkv.shape[0]
+    for start in reversed(range(0, seq, BLOCK)):
+        attention_rows(start, BLOCK, qkv, dout, table, dqkv, acc_k, acc_v, start + BLOCK == seq)
+        count = BLOCK // ROWS
+        units(count, lambda i: terms(start // ROWS + count - 1 - i))
+
+    gbuf[t] = jnp.sum(gsum[...], axis=0, keepdims=True)
+    units(FIRST, lambda u: near(u, ox, u))
+
+    def gain_to(d):
+        return rdma(gbuf.at[t], gbuf.at[t], gs.at[d], gr.at[d], (r, (t + d) % 8))
+
+    for d in range(1, 8):
+        gain_to(d).start()
+    frag_step(7)
 
     def weight_stage(j):
         @pl.when(j == 1)
@@ -507,8 +505,17 @@
         def _():
             frag_step(8)
             for zz in range(nz):
-                for c in range(2):
-                    mean_out(zz, c).start()
+                outer_update(zz)
+
+        @pl.when(j == 10)
+        def _():
+            for d in range(1, 8):
+                ref = gbuf.at[(t + 8 - d) % 8]
+                rdma(ref, ref, gs.at[d], gr.at[d], (r, (t + d) % 8)).wait_recv()
+            total = gbuf[0]
+            for d in range(1, 8):
+                total += gbuf[d]
+            ggain[...] = total / gain[...]
 
         block = depth // STEPS
         at = pl.ds(pl.multiple_of(j * block, block), block)
@@ -518,12 +525,6 @@
         gv[at, :] = g[:, wide_q + HEAD :]
 
     units(STEPS, weight_stage)
-    stores = [(gq, gq_h), (gk, gk_h), (gv, gv_h)]
-    stores = [pltpu.make_async_copy(a, b, store.at[i]) for i, (a, b) in enumerate(stores)]
-    for c in stores:
-        c.start()
-
-    gsum[...] = jnp.zeros_like(gsum)
 
     def finish(u):
         @pl.when(u < FIRST)
@@ -545,30 +546,11 @@
         total = (term(part, mine) + term(from_x, at_x)) + (term(full_p, 5 + u) + term(full_m, 5 + u))
         rows = pl.ds(pl.multiple_of(u * UNIT, UNIT), UNIT)
         xhat, inverse = normalise(rows, tokens)
-        gsum[...] += total * xhat
         scaled = total * gain[...]
         mean = jnp.mean(scaled * xhat, axis=1, keepdims=True)
         gtok[rows, :] = (inverse * (scaled - xhat * mean)).astype(bf)
 
     units(UNITS, finish)
-    gbuf[t] = jnp.sum(gsum[...], axis=0, keepdims=True)
-    out_tokens = pltpu.make_async_copy(gtok, gtok_h, store.at[3])
-    out_tokens.start()
-
-    def gain_to(d):
-        return rdma(gbuf.at[t], gbuf.at[t], gs.at[d], gr.at[d], (r, (t + d) % 8))
-
-    for d in range(1, 8):
-        gain_to(d).start()
-    for d in range(1, 8):
-        ref = gbuf.at[(t + 8 - d) % 8]
-        rdma(ref, ref, gs.at[d], gr.at[d], (r, (t + d) % 8)).wait_recv()
-    total = gbuf[0]
-    for d in range(1, 8):
-        total += gbuf[d]
-    gfin[...] = total
-    out_gain = pltpu.make_async_copy(gfin, ggain_h, store.at[4])
-    out_gain.start()
 
     units(8, lambda i: [gather(w, i, cx, y, i).wait_send() for w in range(3)] and None)
     units(FIRST, lambda i: [gather(w, 8 + i, ox, y, i).wait_send() for w in range(2)] and None)
@@ -586,20 +568,15 @@
     frag_b().wait_send()
     frag_b_back().wait_send()
     frag_a_back().wait_send()
-    for c in stores + [out_tokens, out_gain]:
-        c.wait()
-    for zz in range(nz):
-        for c in range(2):
-            mean_out(zz, c).wait()
-
-
-def run(reps, tokens, gain, wq, wk, wv, dout, global_fragment, local_fragment):
+
+
+def run(reps, tokens, gain, wq, wk, wv, dout, global_fragment, momentum, local_fragment):
     depth = tokens.shape[1]
     seq = dout.shape[0]
     table = rope_constants(seq)
     f32, bf = jnp.float32, jnp.bfloat16
     cols = wq.shape[1] + wk.shape[1] + wv.shape[1]
-    anywhere = pl.BlockSpec(memory_space=pl.ANY)
+    anywhere = pl.BlockSpec(memory_space=pltpu.HBM)
     nz = reps // 4
     zcols = depth // nz
     dma = pltpu.SemaphoreType.DMA
@@ -611,15 +588,15 @@
         vm((seq, depth), bf),
         vm((13 * UNIT, depth), bf), vm((13 * UNIT, depth), bf),
         vm((13 * UNIT, depth // 2), bf), vm((13 * UNIT, depth // 2), bf), vm((17 * UNIT, depth), bf),
-        vm(wq.shape, bf), vm(wk.shape, bf), vm(wv.shape, bf), vm((ROWS, depth), bf),
-        vm((8, 1, depth), f32), vm((UNIT, depth), f32), vm((1, depth), f32),
+        vm((8, 1, depth), f32), vm((8, depth), f32),
         vm((64, depth), bf), vm((32, depth), bf), vm((32, depth), f32), vm((nz, 32, zcols), f32),
         vm((32, zcols), f32), vm((16, zcols), f32), vm((nz, 32, zcols), f32), vm((nz, 32, zcols), f32),
-        vm((16, zcols), f32),
-        dma((9,)), dma((6 + 2 * nz,)),
+        vm((64, depth), f32), vm((64, depth), f32),
+        dma((10,)),
     ]
     scratch += [dma((n,)) for n in (26, 26, 17) * 4]
     scratch += [dma((n,)) for n in (8, 8, 4, 4, nz, nz, nz, nz)]
+    operands = (tokens, gain, wq, wk, wv, dout, table, global_fragment, momentum, local_fragment)
     return pl.pallas_call(
         functools.partial(step_kernel, reps),
         out_shape=(
@@ -629,24 +606,23 @@
             jax.ShapeDtypeStruct((1, depth), f32),
             jax.ShapeDtypeStruct((ROWS, depth), bf),
             jax.ShapeDtypeStruct((64, depth), f32),
+            jax.ShapeDtypeStruct((64, depth), f32),
         ),
-        in_specs=[anywhere] * 9,
-        out_specs=[anywhere] * 6,
+        in_specs=[anywhere] * 10,
+        out_specs=[pl.BlockSpec(memory_space=pltpu.VMEM)] * 7,
         scratch_shapes=scratch,
         compiler_params=pltpu.CompilerParams(
-            vmem_limit_bytes=60 * 1024 * 1024, collective_id=0, has_side_effects=True
+            vmem_limit_bytes=LIMIT, collective_id=0, has_side_effects=True
         ),
-    )(tokens, gain, wq, wk, wv, dout, table, global_fragment, local_fragment)
+    )(*(pltpu.with_memory_space_constraint(a, pltpu.HBM) for a in operands))
 
 
 def body(tokens, norm_gain, w_query, key_weight, value_weight, attention_gradient, global_fragment, momentum, local_fragment):
     replicas = lax.axis_size("rep")
-    gq, gk, gv, grad_gain, grad_tokens, mean = run(
+    gq, gk, gv, grad_gain, grad_tokens, new_global, new_momentum = run(
         replicas, tokens[0], norm_gain, w_query[0], key_weight[0], value_weight[0],
-        attention_gradient[0], global_fragment, local_fragment[0],
+        attention_gradient[0], global_fragment, momentum, local_fragment[0],
     )
-    new_momentum = OUTER_MOMENTUM * momentum + mean
-    new_global = global_fragment - OUTER_RATE * (mean + OUTER_MOMENTUM * new_momentum)
     return (gq[None], gk[None], gv[None], grad_gain, grad_tokens[None], new_global, new_momentum)
 
 

time: 121 us -> 120 us (level)
  other arithmetic: 2.59 us -> 0 us
    sub x1 -> x0, other arithmetic: 2.59 us -> none  [body(): global_fragment - OUTER_RATE * (mean + OUTER_MOMENTUM * new_momentum)]
    unnamed x19 -> x7, local copies, waits for them, and re-layouts: 4.94 us -> 6.14 us
where the time goes in v3:
time: 120 us
  Pallas kernels  113 us (94%)
  local copies, waits for them, and re-layouts  6.14 us (5%)
    pallas_call x1, Pallas kernels, run(): pl.pallas_call(functools.partial(step_kernel, reps), out_shape=(jax.Shape...  113 us
    unnamed x7, local copies, waits for them, and re-layouts  6.14 us

profile of v3, /device:TPU:8, one launch (start us, length us, event | category | flops | bytes accessed | tf_op | source)
XLA Modules:
  0.0 119.8 jit_solution(7282423026279647630)
XLA Ops:
  0.6 113.0 %shard_map.153 = (bf16[3072,256]{1,0:T(8,128)(2,1)S(1)}, bf16[3072,128]{1,0:T(8,128)(2,1)S(1)}, bf16[3072,128]{1,0:T(8,128)(2,1)S(1)}, f32[1,3072]{1,0:T(1,128)S...) custom-call(bf16[128,3072]{1,0:T(8,128)(2,1)} %bitcast.15, f32[1,3072]{1,0:T(1,128)} %gain_h.1, ...), custom_call_target="tpu_custom_call" | custom-call | tf_op jit(solution)/shard_map/pallas_call | solution.py:600
  113.6 1.1 copy.24
  114.8 0.9 copy.25
  115.7 0.9 copy.26
  116.5 0.6 copy.27
  117.1 0.9 copy.28
  118.0 0.9 copy.29
  118.9 0.9 copy.30

commit v4 on v3

--- a/solution.py
+++ b/solution.py
@@ -464,15 +464,33 @@
         def _():
             units(FIRST, lambda u: far_halves(5 * (1 - other) + u, col, u))
 
+    def after_3(i):
+        terms(6 + (far + i) % 2)
+
+    def after_2(i):
+        terms((1 - cx) * (4 + (far + i) % 2) + cx * (4 + far))
+
+    def after_1(i):
+        terms(2 + (far + i) % 2)
+
+    def after_0(i):
+        own = 1 - cx * (1 - (i + 2) // 4)
+        k = (i - cx) * own
+        d = 2 - k + 3 * (k // 2) - 2 * (k // 3)
+        terms(own * (cx * 4 + (y + d) % 4) + (1 - own) * ((far + i) % 2))
+
+        @pl.when(i == 1 + 3 * cx)
+        def _():
+            units(FIRST, lambda u: near(u, ox, u))
+
     seq = qkv.shape[0]
-    for start in reversed(range(0, seq, BLOCK)):
+    after = ((after_0, 4 + cx), (after_1, 2 * cx), (after_2, 2 - cx), (after_3, 2 * (1 - cx)))
+    for b in reversed(range(4)):
+        start = b * BLOCK
         attention_rows(start, BLOCK, qkv, dout, table, dqkv, acc_k, acc_v, start + BLOCK == seq)
-        count = BLOCK // ROWS
-        units(count, lambda i: terms(start // ROWS + count - 1 - i))
+        units(after[b][1], after[b][0])
 
     gbuf[t] = jnp.sum(gsum[...], axis=0, keepdims=True)
-    units(FIRST, lambda u: near(u, ox, u))
-
     def gain_to(d):
         return rdma(gbuf.at[t], gbuf.at[t], gs.at[d], gr.at[d], (r, (t + d) % 8))
 
@@ -481,17 +499,18 @@
     frag_step(7)
 
     def weight_stage(j):
-        @pl.when(j == 1)
+        @pl.when(j == 0)
+        def _():
+            units(3, lambda u: near(5 + u, cx, u))
+
+        @pl.when(j == 3)
+        def _():
+            units(FIRST, across)
+
+        @pl.when(j == 5)
         def _():
             units(later, far_later)
-
-        @pl.when(j == 3)
-        def _():
-            units(FIRST, lambda u: near(5 + u, cx, u))
-
-        @pl.when(j == 5)
-        def _():
-            units(FIRST, across)
+            units(FIRST - 3, lambda u: near(5 + u, cx, u), 3)
 
         @pl.when(j == 7)
         def _():
@@ -617,11 +636,35 @@
     )(*(pltpu.with_memory_space_constraint(a, pltpu.HBM) for a in operands))
 
 
+def flush_kernel(*refs):
+    count = len(refs) // 2
+    sem = refs[-1]
+    copies = [pltpu.make_async_copy(refs[i], refs[count + i], sem.at[i]) for i in range(count)]
+    for c in copies:
+        c.start()
+    for c in copies:
+        c.wait()
+
+
+def flush(*arrays):
+    return pl.pallas_call(
+        flush_kernel,
+        out_shape=tuple(jax.ShapeDtypeStruct(a.shape, a.dtype) for a in arrays),
+        in_specs=[pl.BlockSpec(memory_space=pltpu.VMEM)] * len(arrays),
+        out_specs=[pl.BlockSpec(memory_space=pl.ANY)] * len(arrays),
+        scratch_shapes=[pltpu.SemaphoreType.DMA((len(arrays),))],
+        compiler_params=pltpu.CompilerParams(vmem_limit_bytes=8 * 1024 * 1024),
+    )(*arrays)
+
+
 def body(tokens, norm_gain, w_query, key_weight, value_weight, attention_gradient, global_fragment, momentum, local_fragment):
     replicas = lax.axis_size("rep")
     gq, gk, gv, grad_gain, grad_tokens, new_global, new_momentum = run(
         replicas, tokens[0], norm_gain, w_query[0], key_weight[0], value_weight[0],
         attention_gradient[0], global_fragment, momentum, local_fragment[0],
+    )
+    gq, gk, gv, grad_gain, grad_tokens, new_global, new_momentum = flush(
+        gq, gk, gv, grad_gain, grad_tokens, new_global, new_momentum
     )
     return (gq[None], gk[None], gv[None], grad_gain, grad_tokens[None], new_global, new_momentum)
 

time: 120 us -> 111 us (0.925)
  local copies, waits for them, and re-layouts: 6.14 us -> 0 us
  Pallas kernels: 113 us -> 110 us
    unnamed x7 -> x0, local copies, waits for them, and re-layouts: 6.14 us -> none
    pallas_call x1, Pallas kernels: 113 us -> 108 us  [run(): pl.pallas_call(functools.partial(step_kernel, reps), out_shape=(jax.Shape...]
    pallas_call x0 -> x1, Pallas kernels: none -> 2.5 us  [flush(): pl.pallas_call(flush_kernel, out_shape=tuple((jax.ShapeDtypeStruct(a.shap...]
where the time goes in v4:
time: 111 us
  Pallas kernels  110 us (99%)
    pallas_call x1, Pallas kernels, run(): pl.pallas_call(functools.partial(step_kernel, reps), out_shape=(jax.Shape...  108 us
    pallas_call x1, Pallas kernels, flush(): pl.pallas_call(flush_kernel, out_shape=tuple((jax.ShapeDtypeStruct(a.shap...  2.5 us

profile of v4, /device:TPU:8, one launch (start us, length us, event | category | flops | bytes accessed | tf_op | source)
XLA Modules:
  0.0 111.1 jit_solution(4365785193178329525)
XLA Ops:
  0.6 108.0 %shard_map.153 = (bf16[3072,256]{1,0:T(8,128)(2,1)S(1)}, bf16[3072,128]{1,0:T(8,128)(2,1)S(1)}, bf16[3072,128]{1,0:T(8,128)(2,1)S(1)}, f32[1,3072]{1,0:T(1,128)S...) custom-call(bf16[128,3072]{1,0:T(8,128)(2,1)} %bitcast.11, f32[1,3072]{1,0:T(1,128)} %gain_h.1, ...), custom_call_target="tpu_custom_call" | custom-call | tf_op jit(solution)/shard_map/pallas_call | solution.py:619
  108.6 2.5 %shard_map.154 = (bf16[3072,256]{1,0:T(8,128)(2,1)}, bf16[3072,128]{1,0:T(8,128)(2,1)}, bf16[3072,128]{1,0:T(8,128)(2,1)}, f32[1,3072]{1,0:T(1,128)}, bf16[128,3...) custom-call(bf16[3072,256]{1,0:T(8,128)(2,1)S(1)} %get-tuple-element.21.refs_0_, ...), custom_call_target="tpu_custom_call" | custom-call | tf_op jit(solution)/shard_map/pallas_call | solution.py:650

commit v5 on v4

--- a/solution.py
+++ b/solution.py
@@ -76,11 +76,14 @@
         top = jnp.max(s, axis=0, keepdims=True)
         power = jnp.exp2((s - top) * power_scale)
         inverse = 1.0 / jnp.sum(power, axis=0, keepdims=True)
-        p_low = (power * inverse).astype(jnp.bfloat16)
+        p_low = power.astype(jnp.bfloat16)
         dp = dot_t(values, do)
         drop = jnp.sum(dp * power, axis=0, keepdims=True) * inverse
-        ds = (power * ((dp - drop) * (inverse * scale))).astype(jnp.bfloat16)
-        dq = t_dot(keys, ds).T
+        ds = (power * (dp - drop)).astype(jnp.bfloat16)
+        dq = (t_dot(keys, ds) * (inverse * scale)).T
+        by_row = jnp.broadcast_to(inverse, (HEAD, block)).T
+        do = (do.astype(jnp.float32) * by_row).astype(jnp.bfloat16)
+        q = (q.astype(jnp.float32) * (by_row * scale)).astype(jnp.bfloat16)
         dqkv[rows, h * HEAD : (h + 1) * HEAD] = unrope(dq, cos, sin).astype(jnp.bfloat16)
         tv = jnp.dot(p_low, do, preferred_element_type=jnp.float32)
         tk = jnp.dot(ds, q, preferred_element_type=jnp.float32)
@@ -157,6 +160,12 @@
             device_id=dev, device_id_type=pl.DeviceIdType.MESH,
         )
 
+    barrier = pltpu.get_barrier_semaphore()
+    peers = [(r, (t + d) % 8) for d in range(1, 8)]
+    peers += [dev_core, dev_h] + [rep_dev(xh, (z + d) % nz, core) for d in range(1, nz)]
+    for p in peers:
+        pl.semaphore_signal(barrier, inc=1, device_id=p, device_id_type=pl.DeviceIdType.MESH)
+
     wide_q = wq_h.shape[1]
     loads = [
         (tokens_h, tokens),
@@ -173,12 +182,6 @@
     loads = [pltpu.make_async_copy(a, b, load.at[i]) for i, (a, b) in enumerate(loads)]
     for c in loads:
         c.start()
-
-    barrier = pltpu.get_barrier_semaphore()
-    peers = [(r, (t + d) % 8) for d in range(1, 8)]
-    peers += [dev_core, dev_h] + [rep_dev(xh, (z + d) % nz, core) for d in range(1, nz)]
-    for p in peers:
-        pl.semaphore_signal(barrier, inc=1, device_id=p, device_id_type=pl.DeviceIdType.MESH)
     loads[0].wait()
     loads[1].wait()
 
@@ -498,6 +501,26 @@
         gain_to(d).start()
     frag_step(7)
 
+    def early_sends_ended():
+        units(8, lambda i: [gather(w, i, cx, y, i).wait_send() for w in range(3)] and None)
+        units(FIRST, lambda i: [gather(w, 8 + i, ox, y, i).wait_send() for w in range(2)] and None)
+        units(13, lambda i: [gather(w, 13 + i, cx, y, 0, w).wait_send() for w in range(2)] and None)
+        units(9, lambda i: gather(2, 8 + i, cx, y, 0).wait_send())
+        for d in range(1, 8):
+            gain_to(d).wait_send()
+        for d in range(1, nz):
+            frag_c(d).wait_send()
+            frag_c_back(d).wait_send()
+        frag_a().wait_send()
+        frag_b().wait_send()
+        frag_b_back().wait_send()
+        frag_a_back().wait_send()
+
+    def most_sends_ended():
+        units(13, lambda i: [scatter_half(w, i, cx, y, 0).wait_send() for w in range(2)] and None)
+        units(5 + FIRST, lambda i: [scatter_full(w, i, cx, y, 0).wait_send() for w in range(2)] and None)
+        units(12, lambda i: scatter_x(i, cx, y, 0).wait_send())
+
     def weight_stage(j):
         @pl.when(j == 0)
         def _():
@@ -535,6 +558,7 @@
             for d in range(1, 8):
                 total += gbuf[d]
             ggain[...] = total / gain[...]
+            early_sends_ended()
 
         block = depth // STEPS
         at = pl.ds(pl.multiple_of(j * block, block), block)
@@ -544,6 +568,7 @@
         gv[at, :] = g[:, wide_q + HEAD :]
 
     units(STEPS, weight_stage)
+    most_sends_ended()
 
     def finish(u):
         @pl.when(u < FIRST)
@@ -571,22 +596,8 @@
 
     units(UNITS, finish)
 
-    units(8, lambda i: [gather(w, i, cx, y, i).wait_send() for w in range(3)] and None)
-    units(FIRST, lambda i: [gather(w, 8 + i, ox, y, i).wait_send() for w in range(2)] and None)
-    units(13, lambda i: [gather(w, 13 + i, cx, y, 0, w).wait_send() for w in range(2)] and None)
-    units(9, lambda i: gather(2, 8 + i, cx, y, 0).wait_send())
-    units(13, lambda i: [scatter_full(w, i, cx, y, 0).wait_send() for w in range(2)] and None)
-    units(13, lambda i: [scatter_half(w, i, cx, y, 0).wait_send() for w in range(2)] and None)
-    units(17, lambda i: scatter_x(i, cx, y, 0).wait_send())
-    for d in range(1, 8):
-        gain_to(d).wait_send()
-    for d in range(1, nz):
-        frag_c(d).wait_send()
-        frag_c_back(d).wait_send()
-    frag_a().wait_send()
-    frag_b().wait_send()
-    frag_b_back().wait_send()
-    frag_a_back().wait_send()
+    units(later, lambda i: [scatter_full(w, 5 + FIRST + i, cx, y, 0).wait_send() for w in range(2)] and None)
+    units(FIRST, lambda i: scatter_x(12 + i, cx, y, 0).wait_send())
 
 
 def run(reps, tokens, gain, wq, wk, wv, dout, global_fragment, momentum, local_fragment):

time: 111 us -> 110 us (level)
  no operation moved by 1% of the time
where the time goes in v5:
time: 110 us
  Pallas kernels  110 us (100%)
    pallas_call x1, Pallas kernels, run(): pl.pallas_call(functools.partial(step_kernel, reps), out_shape=(jax.Shape...  107 us
    pallas_call x1, Pallas kernels, flush(): pl.pallas_call(flush_kernel, out_shape=tuple((jax.ShapeDtypeStruct(a.shap...  2.5 us

profile of v5, /device:TPU:8, one launch (start us, length us, event | category | flops | bytes accessed | tf_op | source)
XLA Modules:
  0.0 110.3 jit_solution(8508040998846410669)
XLA Ops:
  0.6 107.1 %shard_map.153 = (bf16[3072,256]{1,0:T(8,128)(2,1)S(1)}, bf16[3072,128]{1,0:T(8,128)(2,1)S(1)}, bf16[3072,128]{1,0:T(8,128)(2,1)S(1)}, f32[1,3072]{1,0:T(1,128)S...) custom-call(bf16[128,3072]{1,0:T(8,128)(2,1)} %bitcast.11, f32[1,3072]{1,0:T(1,128)} %gain_h.1, ...), custom_call_target="tpu_custom_call" | custom-call | tf_op jit(solution)/shard_map/pallas_call | solution.py:630
  107.8 2.5 %shard_map.154 = (bf16[3072,256]{1,0:T(8,128)(2,1)}, bf16[3072,128]{1,0:T(8,128)(2,1)}, bf16[3072,128]{1,0:T(8,128)(2,1)}, f32[1,3072]{1,0:T(1,128)}, bf16[128,3...) custom-call(bf16[3072,256]{1,0:T(8,128)(2,1)S(1)} %get-tuple-element.21.refs_0_, ...), custom_call_target="tpu_custom_call" | custom-call | tf_op jit(solution)/shard_map/pallas_call | solution.py:661

commit v6 on v5

--- a/solution.py
+++ b/solution.py
@@ -105,6 +105,7 @@
 BLOCK = 256
 FIRST = 5
 STEPS = 12
+PIECES = 4
 LIMIT = 44 * 1024 * 1024
 
 
@@ -163,7 +164,7 @@
     barrier = pltpu.get_barrier_semaphore()
     peers = [(r, (t + d) % 8) for d in range(1, 8)]
     peers += [dev_core, dev_h] + [rep_dev(xh, (z + d) % nz, core) for d in range(1, nz)]
-    for p in peers:
+    for p in reversed(peers):
         pl.semaphore_signal(barrier, inc=1, device_id=p, device_id_type=pl.DeviceIdType.MESH)
 
     wide_q = wq_h.shape[1]
@@ -650,7 +651,15 @@
 def flush_kernel(*refs):
     count = len(refs) // 2
     sem = refs[-1]
-    copies = [pltpu.make_async_copy(refs[i], refs[count + i], sem.at[i]) for i in range(count)]
+    copies = []
+    for i in range(count):
+        rows = refs[i].shape[0]
+        piece = rows // PIECES if rows % (16 * PIECES) == 0 else rows
+        for at in range(0, rows, piece):
+            part = slice(at, at + piece)
+            copies.append(
+                pltpu.make_async_copy(refs[i].at[part, :], refs[count + i].at[part, :], sem.at[len(copies)])
+            )
     for c in copies:
         c.start()
     for c in copies:
@@ -663,7 +672,7 @@
         out_shape=tuple(jax.ShapeDtypeStruct(a.shape, a.dtype) for a in arrays),
         in_specs=[pl.BlockSpec(memory_space=pltpu.VMEM)] * len(arrays),
         out_specs=[pl.BlockSpec(memory_space=pl.ANY)] * len(arrays),
-        scratch_shapes=[pltpu.SemaphoreType.DMA((len(arrays),))],
+        scratch_shapes=[pltpu.SemaphoreType.DMA((PIECES * len(arrays),))],
         compiler_params=pltpu.CompilerParams(vmem_limit_bytes=8 * 1024 * 1024),
     )(*arrays)
 

time: 110 us -> 110 us (level)
  no operation moved by 1% of the time
where the time goes in v6:
time: 110 us
  Pallas kernels  110 us (100%)
    pallas_call x1, Pallas kernels, run(): pl.pallas_call(functools.partial(step_kernel, reps), out_shape=(jax.Shape...  107 us
    pallas_call x1, Pallas kernels, flush(): pl.pallas_call(flush_kernel, out_shape=tuple((jax.ShapeDtypeStruct(a.shap...  2.65 us

profile of v6, /device:TPU:8, one launch (start us, length us, event | category | flops | bytes accessed | tf_op | source)
XLA Modules:
  0.0 110.3 jit_solution(16308637274433306832)
XLA Ops:
  0.6 107.0 %shard_map.153 = (bf16[3072,256]{1,0:T(8,128)(2,1)S(1)}, bf16[3072,128]{1,0:T(8,128)(2,1)S(1)}, bf16[3072,128]{1,0:T(8,128)(2,1)S(1)}, f32[1,3072]{1,0:T(1,128)S...) custom-call(bf16[128,3072]{1,0:T(8,128)(2,1)} %bitcast.11, f32[1,3072]{1,0:T(1,128)} %gain_h.1, ...), custom_call_target="tpu_custom_call" | custom-call | tf_op jit(solution)/shard_map/pallas_call | solution.py:631
  107.7 2.6 %shard_map.154 = (bf16[3072,256]{1,0:T(8,128)(2,1)}, bf16[3072,128]{1,0:T(8,128)(2,1)}, bf16[3072,128]{1,0:T(8,128)(2,1)}, f32[1,3072]{1,0:T(1,128)}, bf16[128,3...) custom-call(bf16[3072,256]{1,0:T(8,128)(2,1)S(1)} %get-tuple-element.21.refs_0_, ...), custom_call_target="tpu_custom_call" | custom-call | tf_op jit(solution)/shard_map/pallas_call | solution.py:670
